TPU v7x, 512 devices: a whole 4x8x8 slice. The times are simulated.
512 devices in a mesh: gx: 16 (over y, core), gy: 4 (over x), gz: 8 (over z).
Axes of the slice: x: 4, y: 8, z: 8, core: 2. Of those that a mesh axis runs over, the one named last changes fastest.
Arguments:
- face_blocks: float32 [16, 4, 8, 24, 16384], P('gx', 'gy', 'gz'), may hold values from -6 to 6
- owner_rank: int32 [16, 4, 8, 24, 1], P('gx', 'gy', 'gz'), may hold values from 0 to 15; in each aligned block of 24 rows (0 to 23, 24 to 47, ..., all dimensions but the last counted through in order) at most 2 rows name the same one
- owner_tile: int32 [16, 4, 8, 24], P('gx', 'gy', 'gz'), may hold values from 0 to 31
- live_count: int32 [16, 4, 8], P('gx', 'gy', 'gz'), may hold values from 1 to 24, as said below
- right_side: float32 [256, 256, 1024], P('gx', 'gy', 'gz'), may hold values from -8 to 8
- diagonal: float32 [256, 256, 1024], P('gx', 'gy', 'gz'), may hold values from 0.05 to 1
Outputs:
- solution_field: float32 [256, 256, 1024], P('gx', 'gy', 'gz')
- residual: float32 [256, 256, 1024], P('gx', 'gy', 'gz')
Inputs may be any that keep to these rules, and one draw needn't show every extreme that they name: `owner_rank`: on one device no owner is named by more than 2 of the 24 slots, live or not; some owner is named exactly 2 times on some devices. `live_count`: some device has all 24 slots live in every draw.
All inputs are finite; a program needn't handle non-finite values.
Results may differ from a plain program's by a relative error of at most 0.00012.
Values sent between devices are 32-bit elements; how exact they have to be, the bound alone decides.
A program may use at most 64 MiB of HBM per device.

v0:
```python
import jax
import jax.numpy as jnp
from jax import lax
from jax.sharding import Mesh
from jax.sharding import PartitionSpec as P

BLK = 128
CAP = 2
ITERS = 2
GX_GY_GZ = ("gx_0", "gx_1", "gy", "gz")
GX = ("gx_0", "gx_1")


def padded_2(cells, sides, width):
    for axis, dim in sides:
        count = lax.axis_size(axis)
        ends = count - 1
        head = lax.slice_in_dim(cells, 0, width, axis=dim)
        tail = lax.slice_in_dim(cells, cells.shape[dim] - width, cells.shape[dim], axis=dim)
        cells = jnp.concatenate(
            [
                lax.ppermute(tail, axis, [(i, (i + 1) % count) for i in range(ends)]),
                cells,
                lax.ppermute(head, axis, [((i + 1) % count, i) for i in range(ends)]),
            ],
            axis=dim,
        )
    return cells


def over_axes(value, axes):
    for axis in axes:
        value = lax.psum(value, axis)
    return value


def side_by_side(arrays, axis, split_dim, concat_dim, along):
    columns = [a.reshape(*a.shape[:along], -1) for a in arrays]
    both = jnp.concatenate(columns, axis=along)
    out, at, gathered = (
        lax.all_to_all(both, axis, split_axis=split_dim, concat_axis=concat_dim, tiled=True),
        0,
        [],
    )
    for a, column in zip(arrays, columns):
        share = out[..., at : at + column.shape[along]]
        gathered.append(share.reshape(*share.shape[:along], *a.shape[along:]))
        at += column.shape[along]
    return tuple(gathered)


def restrict(values):
    half = BLK // 2
    shaped = values.reshape(values.shape[:-1] + (half, 2, half, 2))
    summed = 0.25 * jnp.sum(shaped, axis=(-3, -1))
    return summed.reshape(values.shape[:-1] + (half * half,))


def operate(field, diagonal):
    padded = padded_2(field, ((GX, 0), ("gy", 1), ("gz", 2)), 1)
    beside = padded[2:, 1:-1, 1:-1] + padded[:-2, 1:-1, 1:-1]
    beside = beside + padded[1:-1, 2:, 1:-1] + padded[1:-1, :-2, 1:-1]
    beside = beside + padded[1:-1, 1:-1, 2:] + padded[1:-1, 1:-1, :-2]
    return (6.0 + diagonal) * field - beside


def paired(residual, image):
    return (
        over_axes(jnp.sum(residual * residual), GX_GY_GZ),
        over_axes(jnp.sum(residual * image), GX_GY_GZ),
    )


def per_device(face_blocks, owner_rank, owner_tile, live_count, right_side, diagonal):
    block_count = face_blocks.shape[3]
    block_width = face_blocks.shape[4]
    block_rows = face_blocks.reshape(block_count, block_width)
    group_size = lax.axis_size(GX)
    order = jnp.arange(block_count, dtype=jnp.int32)
    living = order < live_count.reshape(())
    target = owner_rank.reshape(block_count)
    before_mask = (
        (target[:, None] == target[None, :]) & (order[None, :] < order[:, None]) & living[None, :]
    )
    position = jnp.sum(before_mask.astype(jnp.int32), axis=1)
    destination_slot = target * CAP + position
    slot_range = jnp.arange(group_size * CAP, dtype=jnp.int32)
    packing = ((destination_slot[None, :] == slot_range[:, None]) & living[None, :]).astype(
        jnp.float32
    )
    tile_labels = (owner_tile.reshape(block_count) + 1).astype(jnp.float32)
    labels = jnp.dot(packing, tile_labels, precision=lax.Precision.HIGHEST).reshape(group_size, CAP)
    packed = jnp.dot(packing, restrict(block_rows), precision=lax.Precision.HIGHEST)
    received, received_tags = side_by_side(
        (packed.reshape(group_size, CAP, -1), labels), GX, 0, 0, 2
    )
    layers = right_side.shape[0]
    incoming = received.reshape(group_size * CAP, -1)
    tag_flat = received_tags.reshape(group_size * CAP)
    tile_range = (jnp.arange(2 * layers, dtype=jnp.int32) + 1).astype(jnp.float32)
    placing = (tag_flat[None, :] == tile_range[:, None]).astype(jnp.float32)
    tile_sums = jnp.dot(placing, incoming, precision=lax.Precision.HIGHEST)
    half = BLK // 2
    source = jnp.transpose(tile_sums.reshape(layers, 2, half, half), (0, 2, 1, 3)).reshape(
        layers, half, 2 * half
    )
    load = right_side + source
    solution_field = jnp.zeros_like(load)
    residual = load
    image = operate(residual, diagonal)
    norm_now, product = paired(residual, image)
    alpha = norm_now / product
    direction, along = (residual, image)
    for iteration in range(ITERS):
        solution_field = solution_field + alpha * direction
        residual = residual - alpha * along
        if iteration + 1 < ITERS:
            image = operate(residual, diagonal)
            norm_next, product = paired(residual, image)
            ratio = norm_next / norm_now
            alpha = norm_next / (product - ratio * norm_next / alpha)
            direction = residual + ratio * direction
            along = image + ratio * along
            norm_now = norm_next
    return (solution_field, residual)


def solution(mesh):
    finer = Mesh(
        mesh.devices.reshape(8, 2, mesh.shape["gy"], mesh.shape["gz"]), ("gx_0", "gx_1", "gy", "gz")
    )
    return jax.shard_map(
        per_device,
        mesh=finer,
        in_specs=(
            P(GX, "gy", "gz", None, None),
            P(GX, "gy", "gz", None, None),
            P(GX, "gy", "gz", None),
            P(GX, "gy", "gz"),
            P(GX, "gy", "gz"),
            P(GX, "gy", "gz"),
        ),
        out_specs=(P(GX, "gy", "gz"), P(GX, "gy", "gz")),
        check_vma=False,
    )
```

profile of v0, /device:TPU:8, one launch (start us, length us, event | category | flops | bytes accessed | tf_op | source)
XLA Modules:
  0.0 210.1 jit_solution(6594678256226598356)
XLA Ops:
  2.9 6.1 %copy.30 = f32[1,1,1,24,16384]{3,4,2,1,0:T(8,128)} copy(f32[1,1,1,24,16384]{4,3,2,1,0:T(8,128)} %param.6) | data formatting | bytes 3145728 | tf_op args[0]
  9.0 9.6 %reduce_sum.55 = f32[24,64,64]{0,2,1:T(8,128)S(1)} reduce(f32[24,64,2,64,2]{0,4,3,2,1:T(2,128)} %bitcast.32, f32[]{:T(128)} %constant.4.clone.1), dimensions={2,4}, to_apply=%region_1.0 | reduce | flops 294912 | bytes 1966084 | tf_op jit(solution)/shard_map/reduce_sum | solution.py:55
  18.8 1.3 fusion.16
  21.5 9.2 %all-to-all-start = ((f32[16,2,4097]{2,1,0:T(2,128)}), f32[16,2,4097]{2,1,0:T(2,128)S(1)}, u32[]{:S(2)}, u32[]{:S(2)}) async-start(f32[16,2,4097]{2,1,0:T(2,128)} %copy.33), calls=%async_computation | async-start | bytes 1081344 | tf_op jit(solution)/shard_map/all_to_all | solution.py:41
  30.7 14.5 %all-to-all-done = f32[16,2,4097]{2,1,0:T(2,128)S(1)} async-done(((f32[16,2,4097]{2,1,0:T(2,128)}), f32[16,2,4097]{2,1,0:T(2,128)S(1)}, u32[]{:S(2)}, u32[]{:S(2)}) %all-to-all-start) | async-done | bytes 524448 | tf_op jit(solution)/shard_map/all_to_all | solution.py:41
  46.2 1.3 convolution_bitcast_fusion
  49.0 5.2 %collective-permute-start = (f32[1,64,128]{2,1,0:T(8,128)S(1)}, f32[1,64,128]{2,1,0:T(8,128)S(1)}, u32[]{:S(2)}, u32[]{:S(2)}) collective-permute-start(f32[1,64,128]{2,1,0:T(8,128)S(1)} %get-tuple-element.37), channel_id=1, source_target_pairs={{32,0},{64,32},{96,64},{128,96},{160,128},{192,160},{224,192},{256... | collective-permute-start | bytes 98312 | tf_op jit(solution)/shard_map/ppermute | solution.py:24
  54.2 1.9 collective-permute-start.1
  56.1 3.3 %collective-permute-done.1 = f32[1,64,128]{2,1,0:T(8,128)S(1)} collective-permute-done((f32[1,64,128]{2,1,0:T(8,128)S(1)}, f32[1,64,128]{2,1,0:T(8,128)S(1)}, u32[]{:S(2)}, u32[]{:S(2)}) %collective-permute-start.1) | collective-permute-done | bytes 32800 | tf_op jit(solution)/shard_map/ppermute | solution.py:22
  59.4 1.3 collective-permute-start.2
  60.7 4.5 %collective-permute-start.3 = (f32[18,1,128]{2,1,0:T(1,128)S(1)}, f32[18,1,128]{2,1,0:T(1,128)S(1)}, u32[]{:S(2)}, u32[]{:S(2)}) collective-permute-start(f32[18,1,128]{2,1,0:T(1,128)S(1)} %get-tuple-element.30), channel_id=1, source_target_pairs={{0,8},{8,16},{16,24},{1,9},{9,17},{17,25},{2,10},{10,18},{18,26},{... | collective-permute-start | bytes 27656 | tf_op jit(solution)/shard_map/ppermute | solution.py:22
  65.3 1.3 collective-permute-done.3
  67.2 1.3 collective-permute-start.4
  68.8 4.6 %collective-permute-start.5 = (f32[18,66,1]{1,2,0:T(1,128)S(1)}, f32[18,66,1]{1,2,0:T(1,128)S(1)}, u32[]{:S(2)}, u32[]{:S(2)}) collective-permute-start(f32[18,66,1]{1,2,0:T(1,128)S(1)} %copy.38), channel_id=1, source_target_pairs={{0,1},{1,2},{2,3},{3,4},{4,5},{5,6},{6,7},{8,9},{9,10},{10,11},{11... | collective-permute-start | bytes 14264 | tf_op jit(solution)/shard_map/ppermute | solution.py:22
  76.3 15.0 %all-reduce.3 = (f32[]{:T(128)}, f32[]{:T(128)}) all-reduce(f32[]{:T(128)} %get-tuple-element.5, f32[]{:T(128)} %get-tuple-element.4), channel_id=1, replica_groups=mesh['gx_0'=8,'gx_1'=2,'gy'=4,'gz'=8] {'gx_0'}, use_global_device_ids=true, to_apply=%region_3.0 | all-reduce | flops 2 | bytes 16 | tf_op jit(solution)/shard_map/psum | solution.py:33
  91.3 3.1 %all-reduce.7 = (f32[]{:T(128)}, f32[]{:T(128)}) all-reduce(f32[]{:T(128)} %get-tuple-element.12, f32[]{:T(128)} %get-tuple-element.13), channel_id=1, replica_groups=mesh['gx_0'=8,'gx_1'=2,'gy'=4,'gz'=8] {'gx_1'}, use_global_device_ids=true, to_apply=%region_4.0 | all-reduce | flops 2 | bytes 16 | tf_op jit(solution)/shard_map/psum | solution.py:33
  94.4 10.9 %all-reduce.5 = (f32[]{:T(128)}, f32[]{:T(128)}) all-reduce(f32[]{:T(128)} %get-tuple-element.20, f32[]{:T(128)} %get-tuple-element.21), channel_id=1, replica_groups=mesh['gx_0'=8,'gx_1'=2,'gy'=4,'gz'=8] {'gy'}, use_global_device_ids=true, to_apply=%region_5.0 | all-reduce | flops 2 | bytes 16 | tf_op jit(solution)/shard_map/psum | solution.py:33
  105.3 24.3 %all-reduce.1 = (f32[]{:T(128)}, f32[]{:T(128)}) all-reduce(f32[]{:T(128)} %get-tuple-element.16, f32[]{:T(128)} %get-tuple-element.17), channel_id=1, replica_groups=mesh['gx_0'=8,'gx_1'=2,'gy'=4,'gz'=8] {'gz'}, use_global_device_ids=true, to_apply=%region_6.0 | all-reduce | flops 2 | bytes 16 | tf_op jit(solution)/shard_map/psum | solution.py:33
  131.1 1.9 collective-permute-start.6
  133.0 2.4 %collective-permute-start.7 = (f32[1,64,128]{2,1,0:T(8,128)S(1)}, f32[1,64,128]{2,1,0:T(8,128)S(1)}, u32[]{:S(2)}, u32[]{:S(2)}) collective-permute-start(f32[1,64,128]{2,1,0:T(8,128)S(1)} %get-tuple-element.34), channel_id=1, source_target_pairs={{0,32},{32,64},{64,96},{96,128},{128,160},{160,192},{192,224},{224... | collective-permute-start | bytes 98312 | tf_op jit(solution)/shard_map/ppermute | solution.py:22
  135.5 2.9 %collective-permute-done.7 = f32[1,64,128]{2,1,0:T(8,128)S(1)} collective-permute-done((f32[1,64,128]{2,1,0:T(8,128)S(1)}, f32[1,64,128]{2,1,0:T(8,128)S(1)}, u32[]{:S(2)}, u32[]{:S(2)}) %collective-permute-start.7) | collective-permute-done | bytes 32800 | tf_op jit(solution)/shard_map/ppermute | solution.py:22
  138.3 1.3 collective-permute-start.8
  139.6 4.5 %collective-permute-start.9 = (f32[18,1,128]{2,1,0:T(1,128)S(1)}, f32[18,1,128]{2,1,0:T(1,128)S(1)}, u32[]{:S(2)}, u32[]{:S(2)}) collective-permute-start(f32[18,1,128]{2,1,0:T(1,128)S(1)} %get-tuple-element.28), channel_id=1, source_target_pairs={{0,8},{8,16},{16,24},{1,9},{9,17},{17,25},{2,10},{10,18},{18,26},{... | collective-permute-start | bytes 27656 | tf_op jit(solution)/shard_map/ppermute | solution.py:22
  144.2 1.3 collective-permute-done.9
  146.1 1.3 collective-permute-start.10
  147.7 4.6 %collective-permute-start.11 = (f32[18,66,1]{1,2,0:T(1,128)S(1)}, f32[18,66,1]{1,2,0:T(1,128)S(1)}, u32[]{:S(2)}, u32[]{:S(2)}) collective-permute-start(f32[18,66,1]{1,2,0:T(1,128)S(1)} %copy.42), channel_id=1, source_target_pairs={{0,1},{1,2},{2,3},{3,4},{4,5},{5,6},{6,7},{8,9},{9,10},{10,11},{11... | collective-permute-start | bytes 14264 | tf_op jit(solution)/shard_map/ppermute | solution.py:22
  154.0 2.1 multiply_reduce_fusion
  156.0 16.3 %all-reduce.2 = (f32[]{:T(128)}, f32[]{:T(128)}) all-reduce(f32[]{:T(128)} %get-tuple-element.3, f32[]{:T(128)} %get-tuple-element.2), channel_id=1, replica_groups=mesh['gx_0'=8,'gx_1'=2,'gy'=4,'gz'=8] {'gx_0'}, use_global_device_ids=true, to_apply=%region_13.0 | all-reduce | flops 2 | bytes 16 | tf_op jit(solution)/shard_map/psum | solution.py:33
  172.4 3.1 %all-reduce.6 = (f32[]{:T(128)}, f32[]{:T(128)}) all-reduce(f32[]{:T(128)} %get-tuple-element.10, f32[]{:T(128)} %get-tuple-element.11), channel_id=1, replica_groups=mesh['gx_0'=8,'gx_1'=2,'gy'=4,'gz'=8] {'gx_1'}, use_global_device_ids=true, to_apply=%region_14.0 | all-reduce | flops 2 | bytes 16 | tf_op jit(solution)/shard_map/psum | solution.py:33
  175.5 10.7 %all-reduce.4 = (f32[]{:T(128)}, f32[]{:T(128)}) all-reduce(f32[]{:T(128)} %get-tuple-element.18, f32[]{:T(128)} %get-tuple-element.19), channel_id=1, replica_groups=mesh['gx_0'=8,'gx_1'=2,'gy'=4,'gz'=8] {'gy'}, use_global_device_ids=true, to_apply=%region_15.0 | all-reduce | flops 2 | bytes 16 | tf_op jit(solution)/shard_map/psum | solution.py:33
  186.2 17.1 %all-reduce = (f32[]{:T(128)}, f32[]{:T(128)}) all-reduce(f32[]{:T(128)} %get-tuple-element.14, f32[]{:T(128)} %get-tuple-element.15), channel_id=1, replica_groups=mesh['gx_0'=8,'gx_1'=2,'gy'=4,'gz'=8] {'gz'}, use_global_device_ids=true, to_apply=%region_16.0 | all-reduce | flops 2 | bytes 16 | tf_op jit(solution)/shard_map/psum | solution.py:33
  207.8 2.2 %multiply_subtract_fusion = (f32[16,64,128]{2,1,0:T(8,128)}, f32[16,64,128]{2,1,0:T(8,128)}) fusion(f32[16,64,128]{2,1,0:T(8,128)S(1)} %multiply_subtract_fusion.1, f32[16,64,128]{2,1,0:T(8,128)} %get-tuple-element.22, f32[16,64,128]{2,1,0:T(8,128)S(1)} %get-tuple-element.23, f32[]{:T(128)S(6)} %div.13, f32[]{:T(128)S(6)} %div.15, ...), kind=kLoop, calls=%fused_computation.56 | loop fusion | flops 1179648 | bytes 3145740 | tf_op jit(solution)/shard_map/sub | solution.py:116
  (49 shorter events, 12.0 us)
Async XLA Ops:
  18.8 1.4 copy-start.2
  21.5 23.7 %all-to-all-start = ((f32[16,2,4097]{2,1,0:T(2,128)}), f32[16,2,4097]{2,1,0:T(2,128)S(1)}, u32[]{:S(2)}, u32[]{:S(2)}) async-start(f32[16,2,4097]{2,1,0:T(2,128)} %copy.33), calls=%async_computation | async-start | bytes 1081344 | tf_op jit(solution)/shard_map/all_to_all | solution.py:41
  47.5 1.4 copy-start.1
  49.0 7.1 %collective-permute-start = (f32[1,64,128]{2,1,0:T(8,128)S(1)}, f32[1,64,128]{2,1,0:T(8,128)S(1)}, u32[]{:S(2)}, u32[]{:S(2)}) collective-permute-start(f32[1,64,128]{2,1,0:T(8,128)S(1)} %get-tuple-element.37), channel_id=1, source_target_pairs={{32,0},{64,32},{96,64},{128,96},{160,128},{192,160},{224,192},{256... | collective-permute-start | bytes 98312 | tf_op jit(solution)/shard_map/ppermute | solution.py:24
  54.2 5.2 %collective-permute-start.1 = (f32[1,64,128]{2,1,0:T(8,128)S(1)}, f32[1,64,128]{2,1,0:T(8,128)S(1)}, u32[]{:S(2)}, u32[]{:S(2)}) collective-permute-start(f32[1,64,128]{2,1,0:T(8,128)S(1)} %get-tuple-element.36), channel_id=1, source_target_pairs={{0,32},{32,64},{64,96},{96,128},{128,160},{160,192},{192,224},{224... | collective-permute-start | bytes 98312 | tf_op jit(solution)/shard_map/ppermute | solution.py:22
  59.4 5.9 %collective-permute-start.2 = (f32[18,1,128]{2,1,0:T(1,128)S(1)}, f32[18,1,128]{2,1,0:T(1,128)S(1)}, u32[]{:S(2)}, u32[]{:S(2)}) collective-permute-start(f32[18,1,128]{2,1,0:T(1,128)S(1)} %get-tuple-element.31), channel_id=1, source_target_pairs={{8,0},{16,8},{24,16},{9,1},{17,9},{25,17},{10,2},{18,10},{26,18},{... | collective-permute-start | bytes 27656 | tf_op jit(solution)/shard_map/ppermute | solution.py:24
  60.7 5.9 %collective-permute-start.3 = (f32[18,1,128]{2,1,0:T(1,128)S(1)}, f32[18,1,128]{2,1,0:T(1,128)S(1)}, u32[]{:S(2)}, u32[]{:S(2)}) collective-permute-start(f32[18,1,128]{2,1,0:T(1,128)S(1)} %get-tuple-element.30), channel_id=1, source_target_pairs={{0,8},{8,16},{16,24},{1,9},{9,17},{17,25},{2,10},{10,18},{18,26},{... | collective-permute-start | bytes 27656 | tf_op jit(solution)/shard_map/ppermute | solution.py:22
  66.7 8.4 %copy-start = (f32[16,64,128]{2,1,0:T(8,128)S(1)}, f32[16,64,128]{2,1,0:T(8,128)}, u32[]{:S(2)}) copy-start(f32[16,64,128]{2,1,0:T(8,128)} %param.11) | copy-start | bytes 1572868
  67.2 6.1 %collective-permute-start.4 = (f32[18,66,1]{1,2,0:T(1,128)S(1)}, f32[18,66,1]{1,2,0:T(1,128)S(1)}, u32[]{:S(2)}, u32[]{:S(2)}) collective-permute-start(f32[18,66,1]{1,2,0:T(1,128)S(1)} %copy.36), channel_id=1, source_target_pairs={{1,0},{2,1},{3,2},{4,3},{5,4},{6,5},{7,6},{9,8},{10,9},{11,10},{12... | collective-permute-start | bytes 14264 | tf_op jit(solution)/shard_map/ppermute | solution.py:24
  68.8 5.9 %collective-permute-start.5 = (f32[18,66,1]{1,2,0:T(1,128)S(1)}, f32[18,66,1]{1,2,0:T(1,128)S(1)}, u32[]{:S(2)}, u32[]{:S(2)}) collective-permute-start(f32[18,66,1]{1,2,0:T(1,128)S(1)} %copy.38), channel_id=1, source_target_pairs={{0,1},{1,2},{2,3},{3,4},{4,5},{5,6},{6,7},{8,9},{9,10},{10,11},{11... | collective-permute-start | bytes 14264 | tf_op jit(solution)/shard_map/ppermute | solution.py:22
  131.1 4.3 %collective-permute-start.6 = (f32[1,64,128]{2,1,0:T(8,128)S(1)}, f32[1,64,128]{2,1,0:T(8,128)S(1)}, u32[]{:S(2)}, u32[]{:S(2)}) collective-permute-start(f32[1,64,128]{2,1,0:T(8,128)S(1)} %get-tuple-element.35), channel_id=1, source_target_pairs={{32,0},{64,32},{96,64},{128,96},{160,128},{192,160},{224,192},{256... | collective-permute-start | bytes 98312 | tf_op jit(solution)/shard_map/ppermute | solution.py:24
  133.0 5.3 %collective-permute-start.7 = (f32[1,64,128]{2,1,0:T(8,128)S(1)}, f32[1,64,128]{2,1,0:T(8,128)S(1)}, u32[]{:S(2)}, u32[]{:S(2)}) collective-permute-start(f32[1,64,128]{2,1,0:T(8,128)S(1)} %get-tuple-element.34), channel_id=1, source_target_pairs={{0,32},{32,64},{64,96},{96,128},{128,160},{160,192},{192,224},{224... | collective-permute-start | bytes 98312 | tf_op jit(solution)/shard_map/ppermute | solution.py:22
  138.3 5.9 %collective-permute-start.8 = (f32[18,1,128]{2,1,0:T(1,128)S(1)}, f32[18,1,128]{2,1,0:T(1,128)S(1)}, u32[]{:S(2)}, u32[]{:S(2)}) collective-permute-start(f32[18,1,128]{2,1,0:T(1,128)S(1)} %get-tuple-element.29), channel_id=1, source_target_pairs={{8,0},{16,8},{24,16},{9,1},{17,9},{25,17},{10,2},{18,10},{26,18},{... | collective-permute-start | bytes 27656 | tf_op jit(solution)/shard_map/ppermute | solution.py:24
  139.6 5.9 %collective-permute-start.9 = (f32[18,1,128]{2,1,0:T(1,128)S(1)}, f32[18,1,128]{2,1,0:T(1,128)S(1)}, u32[]{:S(2)}, u32[]{:S(2)}) collective-permute-start(f32[18,1,128]{2,1,0:T(1,128)S(1)} %get-tuple-element.28), channel_id=1, source_target_pairs={{0,8},{8,16},{16,24},{1,9},{9,17},{17,25},{2,10},{10,18},{18,26},{... | collective-permute-start | bytes 27656 | tf_op jit(solution)/shard_map/ppermute | solution.py:22
  146.1 6.1 %collective-permute-start.10 = (f32[18,66,1]{1,2,0:T(1,128)S(1)}, f32[18,66,1]{1,2,0:T(1,128)S(1)}, u32[]{:S(2)}, u32[]{:S(2)}) collective-permute-start(f32[18,66,1]{1,2,0:T(1,128)S(1)} %copy.40), channel_id=1, source_target_pairs={{1,0},{2,1},{3,2},{4,3},{5,4},{6,5},{7,6},{9,8},{10,9},{11,10},{12... | collective-permute-start | bytes 14264 | tf_op jit(solution)/shard_map/ppermute | solution.py:24
  147.7 5.9 %collective-permute-start.11 = (f32[18,66,1]{1,2,0:T(1,128)S(1)}, f32[18,66,1]{1,2,0:T(1,128)S(1)}, u32[]{:S(2)}, u32[]{:S(2)}) collective-permute-start(f32[18,66,1]{1,2,0:T(1,128)S(1)} %copy.42), channel_id=1, source_target_pairs={{0,1},{1,2},{2,3},{3,4},{4,5},{5,6},{6,7},{8,9},{9,10},{10,11},{11... | collective-permute-start | bytes 14264 | tf_op jit(solution)/shard_map/ppermute | solution.py:22
where the time goes:
time: 211 us; the launch traced here: 210 us
  blocking collectives  101 us (48%)
  starting transfers between devices  43.9 us (21%)
  waiting for transfers between devices  25.4 us (12%)
  other arithmetic  17.3 us (8%)
  local copies, waits for them, and re-layouts  12.5 us (6%)
  between operations  7.58 us (4%)
  matrix products  2.81 us (1%)
    psum x8, blocking collectives, over_axes(): value = lax.psum(value, axis)  101 us
    ppermute x6, starting transfers between devices, padded_2(): lax.ppermute(tail, axis, [(i, (i + 1) % count) for i in range(ends)])  22.5 us
    all_to_all x1, waiting for transfers between devices, side_by_side(): lax.all_to_all(both, axis, split_axis=split_dim, concat_axis=concat_dim,...  14.5 us
    ppermute x6, starting transfers between devices, padded_2(): lax.ppermute(head, axis, [((i + 1) % count, i) for i in range(ends)])  12.2 us
    ppermute x6, waiting for transfers between devices, padded_2(): lax.ppermute(tail, axis, [(i, (i + 1) % count) for i in range(ends)])  10.9 us
    reduce_sum x1, other arithmetic, restrict(): summed = 0.25 * jnp.sum(shaped, axis=(-3, -1))  9.6 us
    all_to_all x1, starting transfers between devices, side_by_side(): lax.all_to_all(both, axis, split_axis=split_dim, concat_axis=concat_dim,...  9.17 us
    unnamed x7, local copies, waits for them, and re-layouts  6.11 us
  transfers between devices with their start and end apart: 13, of which 7 were waited for; matrix products, arithmetic and copies ran while one was open for 1% of the time, Pallas kernels for 0%

commit v1 on v0

v1 whole, which is shorter than its diff:
```python
import functools

import jax
import jax.numpy as jnp
from jax import lax
from jax.experimental import pallas as pl
from jax.experimental.pallas import tpu as pltpu
from jax.sharding import PartitionSpec as P

NB = 24
BLK = 128
HALF = BLK // 2
CX = 16
F32 = jnp.float32
MESH = pl.DeviceIdType.MESH
TOP = 8


def body(
    n_gx, n_gy, n_gz,
    count_hbm, rank_hbm, tile_hbm, face_ref, rhs_ref, diag_ref,
    x_out, r_out,
    count_ref, rank_ref, tile_ref, live_rank, face, rows, pair, sbuf, rbuf, stag, rtag,
    v0, v1, v2, diag, ysend, yrecv, zsend, zrecv,
    part_a, part_b, recv_a, recv_b,
    in_sem, s_sem, r_sem, st_sem, rt_sem, hs_sem, hr_sem,
    as_sem, ar_sem, bs_sem, br_sem,
):
    gx, gy, gz = lax.axis_index("gx"), lax.axis_index("gy"), lax.axis_index("gz")
    chips = n_gx // 2
    chip, core = gx // 2, gx % 2
    plane_n = n_gy * n_gz
    plane_me = gy * n_gz + gz
    barrier = pltpu.get_barrier_semaphore()

    small_copies = [
        pltpu.make_async_copy(src, dst, in_sem.at[6 + i])
        for i, (src, dst) in enumerate(
            ((count_hbm, count_ref), (rank_hbm, rank_ref), (tile_hbm, tile_ref))
        )
    ]
    for c in small_copies:
        c.start()
    pieces = 4
    width = face.shape[1] // pieces
    face_copies = [
        pltpu.make_async_copy(
            face_ref.at[:, pl.ds(i * width, width)], face.at[:, pl.ds(i * width, width)], in_sem.at[i]
        )
        for i in range(pieces)
    ]
    for c in face_copies:
        c.start()
    rhs_copy = pltpu.make_async_copy(
        rhs_ref, v0.at[pl.ds(1, CX), pl.ds(TOP, HALF), :], in_sem.at[pieces]
    )
    rhs_copy.start()
    diag_copy = pltpu.make_async_copy(diag_ref, diag, in_sem.at[pieces + 1])
    diag_copy.start()

    zrecv[...] = jnp.zeros_like(zrecv)
    yrecv[...] = jnp.zeros_like(yrecv)

    @pl.loop(1, n_gx)
    def _(k):
        pl.semaphore_signal(
            barrier, inc=1, device_id=(lax.rem(gx + k, n_gx), gy, gz), device_id_type=MESH
        )

    def plane_peer(k):
        q = lax.rem(plane_me + k, plane_n)
        return q // n_gz, lax.rem(q, n_gz)

    @pl.loop(1, plane_n)
    def _(k):
        py, pz = plane_peer(k)
        pl.semaphore_signal(barrier, inc=1, device_id=(gx, py, pz), device_id_type=MESH)

    lane = lax.broadcasted_iota(jnp.int32, (8, BLK), 1)
    k_at = lax.broadcasted_iota(jnp.int32, (2 * BLK, BLK), 0)
    c_at = lax.broadcasted_iota(jnp.int32, (2 * BLK, BLK), 1)
    hit = (k_at // BLK == c_at // HALF) & ((k_at % BLK) // 2 == c_at % HALF)
    pair[...] = jnp.where(hit, 0.25, 0.0).astype(jnp.bfloat16)
    rows[NB] = jnp.zeros((HALF, BLK), F32)
    by_row = rows.reshape((NB + 1) * HALF, BLK)
    for c in small_copies:
        c.wait()
    count = count_ref[0]
    for s in range(NB):
        live_rank[s] = jnp.where(s < count, rank_ref[s], -1)

    pl.semaphore_wait(barrier, n_gx - 1 + plane_n - 1)

    @pl.when(gx == 0)
    def _():
        for v in (v0, v1):
            v[0, pl.ds(TOP, HALF), :] = jnp.zeros((HALF, BLK), F32)

    @pl.when(gx == n_gx - 1)
    def _():
        for v in (v0, v1):
            v[CX + 1, pl.ds(TOP, HALF), :] = jnp.zeros((HALF, BLK), F32)

    per = HALF // pieces
    for i in range(pieces):
        face_copies[i].wait()

        @pl.loop(0, per // 4)
        def _(r4):
            for u in range(4):
                r = i * per + r4 * 4 + u
                at = pl.multiple_of(r * 2 * BLK, 2 * BLK)
                both = face[:, pl.ds(at, BLK)] + face[:, pl.ds(at + BLK, BLK)]
                for g in range(NB // 8):
                    by_row[pl.ds(g * 8 * HALF + r, 8, stride=HALF), :] = both[g * 8 : g * 8 + 8]

    def step_chip(t):
        j = t // 2
        return (1 - 2 * (j % 2)) * (chips // 2 - (j + 1) // 2)

    def target_of(t):
        return lax.rem(chip + step_chip(t) + chips, chips) * 2 + lax.rem(core + 1 + t, 2)

    def source_of(t):
        return lax.rem(chip - step_chip(t) + chips, chips) * 2 + lax.rem(core + 1 + t, 2)

    def packed(tgt):
        i0, i1 = jnp.int32(NB), jnp.int32(NB)
        l0, l1 = jnp.int32(0), jnp.int32(0)
        for s in range(NB):
            named = live_rank[s] == tgt
            label = tile_ref[s] + 1
            free = i0 == NB
            first = named & free
            second = named & jnp.logical_not(free)
            i1 = jnp.where(second, s, i1)
            l1 = jnp.where(second, label, l1)
            i0 = jnp.where(first, s, i0)
            l0 = jnp.where(first, label, l0)
        a = rows[i0]
        b = rows[i1]
        w = jnp.concatenate([a, b], axis=1)
        hi = w.astype(jnp.bfloat16)
        rest = w - hi.astype(F32)
        mid = rest.astype(jnp.bfloat16)
        low = (rest - mid.astype(F32)).astype(jnp.bfloat16)
        s = pair[...]
        o = jnp.dot(hi, s, preferred_element_type=F32)
        o = o + jnp.dot(mid, s, preferred_element_type=F32)
        o = o + jnp.dot(low, s, preferred_element_type=F32)
        tag = jnp.where(lane[0:1] < HALF, l0, l1).astype(F32)
        return o, tag

    def tile_copy(t, tgt, slot):
        return pltpu.make_async_remote_copy(
            src_ref=sbuf.at[t], dst_ref=rbuf.at[slot], send_sem=s_sem.at[t], recv_sem=r_sem.at[slot],
            device_id=(tgt, gy, gz), device_id_type=MESH,
        )

    def tag_copy(t, tgt, slot):
        return pltpu.make_async_remote_copy(
            src_ref=stag.at[t], dst_ref=rtag.at[slot], send_sem=st_sem.at[t], recv_sem=rt_sem.at[slot],
            device_id=(tgt, gy, gz), device_id_type=MESH,
        )

    @pl.loop(0, n_gx - 1)
    def _(t):
        tgt = target_of(t)
        o, tag = packed(tgt)
        stag[t] = tag
        sbuf[t] = o
        tag_copy(t, tgt, gx).start()
        tile_copy(t, tgt, gx).start()

    def add_tiles(tile, tag):
        swapped = pltpu.roll(tile, HALF, 1)
        tag = jnp.broadcast_to(tag, (8, BLK))
        tag_swapped = pltpu.roll(tag, HALF, 1)[0:1]
        tag = tag[0:1]
        want = (lane[0:1] // HALF + 1).astype(F32)

        @pl.loop(0, CX // 4)
        def _(x4):
            for u in range(4):
                x = x4 * 4 + u
                here = want + (2 * x).astype(F32)
                m = jnp.broadcast_to(tag == here, (HALF, BLK))
                ms = jnp.broadcast_to(tag_swapped == here, (HALF, BLK))
                more = jnp.where(m, tile, 0.0) + jnp.where(ms, swapped, 0.0)
                v0[1 + x, pl.ds(TOP, HALF), :] = v0[1 + x, pl.ds(TOP, HALF), :] + more

    rhs_copy.wait()
    own, own_tag = packed(gx)
    add_tiles(own, own_tag)

    @pl.loop(0, n_gx - 1)
    def _(t):
        src = source_of(t)
        tag_copy(t, src, src).wait_recv()
        tile_copy(t, src, src).wait_recv()
        add_tiles(rbuf[src], rtag[src])

    diag_copy.wait()

    ends = (lane == 0) | (lane == BLK - 1)
    even = lane % 2 == 0
    inner = pl.ds(TOP, HALF)

    def halo(v, at):
        def x_down():
            return pltpu.make_async_remote_copy(
                src_ref=v.at[1, inner, :], dst_ref=v.at[CX + 1, inner, :],
                send_sem=hs_sem.at[at, 0], recv_sem=hr_sem.at[at, 0],
                device_id=(gx - 1, gy, gz), device_id_type=MESH,
            )

        def x_up():
            return pltpu.make_async_remote_copy(
                src_ref=v.at[CX, inner, :], dst_ref=v.at[0, inner, :],
                send_sem=hs_sem.at[at, 1], recv_sem=hr_sem.at[at, 1],
                device_id=(gx + 1, gy, gz), device_id_type=MESH,
            )

        def y_down():
            return pltpu.make_async_remote_copy(
                src_ref=ysend.at[at, 0], dst_ref=yrecv.at[at, 0],
                send_sem=hs_sem.at[at, 2], recv_sem=hr_sem.at[at, 2],
                device_id=(gx, gy - 1, gz), device_id_type=MESH,
            )

        def y_up():
            return pltpu.make_async_remote_copy(
                src_ref=ysend.at[at, 1], dst_ref=yrecv.at[at, 1],
                send_sem=hs_sem.at[at, 3], recv_sem=hr_sem.at[at, 3],
                device_id=(gx, gy + 1, gz), device_id_type=MESH,
            )

        def z_down():
            return pltpu.make_async_remote_copy(
                src_ref=zsend.at[at, 0], dst_ref=zrecv.at[at, 0],
                send_sem=hs_sem.at[at, 4], recv_sem=hr_sem.at[at, 4],
                device_id=(gx, gy, gz - 1), device_id_type=MESH,
            )

        def z_up():
            return pltpu.make_async_remote_copy(
                src_ref=zsend.at[at, 1], dst_ref=zrecv.at[at, 1],
                send_sem=hs_sem.at[at, 5], recv_sem=hr_sem.at[at, 5],
                device_id=(gx, gy, gz + 1), device_id_type=MESH,
            )

        return (
            (x_down, gx > 0, gx < n_gx - 1),
            (x_up, gx < n_gx - 1, gx > 0),
            (y_down, gy > 0, gy < n_gy - 1),
            (y_up, gy < n_gy - 1, gy > 0),
            (z_down, gz > 0, gz < n_gz - 1),
            (z_up, gz < n_gz - 1, gz > 0),
        )

    def send_faces(v, at):
        faces = halo(v, at)

        def go(which):
            for copy, sends, _ in which:
                @pl.when(sends)
                def _():
                    copy().start()

        go(faces[:2])
        for p in range(CX):
            ysend[at, 0, pl.ds(p, 1), :] = v[1 + p, pl.ds(TOP, 1), :]
            ysend[at, 1, pl.ds(p, 1), :] = v[1 + p, pl.ds(TOP + HALF - 1, 1), :]
        go(faces[2:4])

        def gather(i, carry):
            out = []
            for u in range(2):
                p = 2 * i + u
                acc = None
                for yb in range(HALF // 8):
                    c = jnp.where(ends, v[1 + p, pl.ds(TOP + 8 * yb, 8), :], 0.0)
                    if yb:
                        c = pltpu.roll(c, 16 * yb, 1)
                    acc = c if acc is None else acc + c
                out.append(carry[u] + pltpu.roll(acc, p, 1))
            return tuple(out)

        zero = jnp.zeros((8, BLK), F32)
        v_even, v_odd = lax.fori_loop(0, CX // 2, gather, (zero, zero))
        zsend[at, 0] = jnp.where(even, v_even, v_odd)
        zsend[at, 1] = jnp.where(even, v_odd, v_even)
        go(faces[4:])

    def take_faces(v, at):
        for copy, _, receives in halo(v, at):
            @pl.when(receives)
            def _():
                copy().wait_recv()
        for p in range(CX):
            v[1 + p, pl.ds(TOP + HALF, 1), :] = yrecv[at, 0, pl.ds(p, 1), :]
            v[1 + p, pl.ds(TOP - 1, 1), :] = yrecv[at, 1, pl.ds(p, 1), :]
        right, left = zrecv[at, 0], zrecv[at, 1]
        return jnp.where(even, right, left), jnp.where(even, left, right)

    def apply(v, at, visit, sums):
        sides = take_faces(v, at)

        def planes(i, sums):
            for u in range(2):
                p = 2 * i + u
                side = pltpu.roll(sides[u], lax.rem(BLK - p, BLK), 1)
                for yb in range(HALF // 8):
                    row = TOP + 8 * yb
                    h = pltpu.roll(side, BLK - 16 * yb, 1) if yb else side
                    c = v[1 + p, pl.ds(row, 8), :]
                    near = v[p, pl.ds(row, 8), :] + v[2 + p, pl.ds(row, 8), :]
                    near = near + (v[1 + p, pl.ds(row - 1, 8), :] + v[1 + p, pl.ds(row + 1, 8), :])
                    z_low = pltpu.roll(jnp.where(lane == BLK - 1, h, c), 1, 1)
                    z_high = pltpu.roll(jnp.where(lane == 0, h, c), BLK - 1, 1)
                    near = near + (z_low + z_high)
                    image = (6.0 + diag[p, pl.ds(8 * yb, 8), :]) * c - near
                    sums = visit(p, yb, c, image, sums)
            return sums

        return lax.fori_loop(0, CX // 2, planes, sums)

    zero = jnp.zeros((8, BLK), F32)

    def visit_1(p, yb, c, image, sums):
        v1[1 + p, pl.ds(TOP + 8 * yb, 8), :] = image
        return sums[0] + c * c, sums[1] + c * image, sums[2] + image * image

    def visit_2(p, yb, c, image, sums):
        v2[p, pl.ds(8 * yb, 8), :] = image
        return sums + c * image

    send_faces(v0, 0)
    m0, m1, m2 = apply(v0, 0, visit_1, (zero, zero, zero))
    send_faces(v1, 1)
    m3 = apply(v1, 1, visit_2, zero)

    quarter = lane // 32
    folded = []
    for m in (m0, m1, m2, m3):
        m = m + pltpu.roll(m, 64, 1)
        folded.append(m + pltpu.roll(m, 32, 1))
    mine = jnp.where(
        quarter == 0, folded[0],
        jnp.where(quarter == 1, folded[1], jnp.where(quarter == 2, folded[2], folded[3])),
    )
    mine = mine + pltpu.roll(mine, 4, 0)
    mine = mine + pltpu.roll(mine, 2, 0)
    mine = mine + pltpu.roll(mine, 1, 0)
    part_a[...] = mine[0:1]

    def a_copy(k, peer, slot):
        return pltpu.make_async_remote_copy(
            src_ref=part_a, dst_ref=recv_a.at[slot], send_sem=as_sem.at[k], recv_sem=ar_sem.at[slot],
            device_id=(peer, gy, gz), device_id_type=MESH,
        )

    def b_copy(k, peer, slot):
        return pltpu.make_async_remote_copy(
            src_ref=part_b, dst_ref=recv_b.at[slot], send_sem=bs_sem.at[k], recv_sem=br_sem.at[slot],
            device_id=(gx,) + peer, device_id_type=MESH,
        )

    def total(refs):
        while len(refs) > 1:
            refs = [refs[i] + refs[i + 1] if i + 1 < len(refs) else refs[i] for i in range(0, len(refs), 2)]
        return refs[0]

    @pl.loop(1, n_gx)
    def _(k):
        a_copy(k, lax.rem(gx + k, n_gx), gx).start()

    recv_a[gx] = mine[0:1]

    @pl.loop(1, n_gx)
    def _(k):
        src = lax.rem(gx + k, n_gx)
        a_copy(k, src, src).wait_recv()

    stage = total([recv_a[i] for i in range(n_gx)])
    part_b[...] = stage

    @pl.loop(1, plane_n)
    def _(k):
        b_copy(k, plane_peer(k), plane_me).start()

    recv_b[plane_me] = stage

    @pl.loop(1, plane_n)
    def _(k):
        py, pz = plane_peer(k)
        b_copy(k, (py, pz), py * n_gz + pz).wait_recv()

    whole = jnp.broadcast_to(total([recv_b[i] for i in range(plane_n)]), (8, BLK))
    for shift in (16, 8, 4, 2, 1):
        whole = whole + pltpu.roll(whole, shift, 1)
    m0, m1, m2, m3 = (
        jnp.broadcast_to(whole[:, 32 * q + 31 : 32 * q + 32], (8, BLK)) for q in range(4)
    )
    alpha_0 = m0 / m1
    square = alpha_0 * alpha_0
    grown = square * m2 / m0
    alpha_1 = (grown - 1.0) * m0 / (square * m3 - grown * grown * m1)
    c0 = alpha_0 + alpha_1 * grown
    c1 = alpha_0 * alpha_1

    @pl.loop(0, CX)
    def _(p):
        for yb in range(HALF // 8):
            a = v0[1 + p, pl.ds(TOP + 8 * yb, 8), :]
            b = v1[1 + p, pl.ds(TOP + 8 * yb, 8), :]
            c = v2[p, pl.ds(8 * yb, 8), :]
            x_out[p, pl.ds(8 * yb, 8), :] = c0 * a - c1 * b
            r_out[p, pl.ds(8 * yb, 8), :] = a - c0 * b + c1 * c

    @pl.loop(0, n_gx - 1)
    def _(t):
        tag_copy(t, target_of(t), gx).wait_send()
        tile_copy(t, target_of(t), gx).wait_send()

    for v, at in ((v0, 0), (v1, 1)):
        for copy, sends, _ in halo(v, at):
            @pl.when(sends)
            def _():
                copy().wait_send()

    @pl.loop(1, n_gx)
    def _(k):
        a_copy(k, lax.rem(gx + k, n_gx), gx).wait_send()

    @pl.loop(1, plane_n)
    def _(k):
        b_copy(k, plane_peer(k), plane_me).wait_send()


def per_device(sizes, face_blocks, owner_rank, owner_tile, live_count, right_side, diagonal):
    n_gx, n_gy, n_gz = sizes
    plane_n = n_gy * n_gz
    box = (CX, HALF, BLK)
    padded = (CX + 2, HALF + 2 * TOP, BLK)
    vmem = pl.BlockSpec(memory_space=pltpu.VMEM)
    hbm = pl.BlockSpec(memory_space=pltpu.HBM)
    dma, scratch = pltpu.SemaphoreType.DMA, pltpu.VMEM
    return pl.pallas_call(
        functools.partial(body, n_gx, n_gy, n_gz),
        out_shape=(jax.ShapeDtypeStruct(box, F32), jax.ShapeDtypeStruct(box, F32)),
        in_specs=[hbm] * 6,
        out_specs=(vmem, vmem),
        scratch_shapes=[
            pltpu.SMEM((1,), jnp.int32),
            pltpu.SMEM((NB,), jnp.int32),
            pltpu.SMEM((NB,), jnp.int32),
            pltpu.SMEM((NB,), jnp.int32),
            scratch((NB, BLK * BLK), F32),
            scratch((NB + 1, HALF, BLK), F32),
            scratch((2 * BLK, BLK), jnp.bfloat16),
            scratch((n_gx, HALF, BLK), F32),
            scratch((n_gx, HALF, BLK), F32),
            scratch((n_gx, 1, BLK), F32),
            scratch((n_gx, 1, BLK), F32),
            scratch(padded, F32),
            scratch(padded, F32),
            scratch(box, F32),
            scratch(box, F32),
            scratch((2, 2, CX, BLK), F32),
            scratch((2, 2, CX, BLK), F32),
            scratch((2, 2, 8, BLK), F32),
            scratch((2, 2, 8, BLK), F32),
            scratch((1, BLK), F32),
            scratch((1, BLK), F32),
            scratch((n_gx, 1, BLK), F32),
            scratch((plane_n, 1, BLK), F32),
            dma((9,)),
            dma((n_gx,)), dma((n_gx,)), dma((n_gx,)), dma((n_gx,)),
            dma((2, 6)), dma((2, 6)),
            dma((n_gx,)), dma((n_gx,)), dma((plane_n,)), dma((plane_n,)),
        ],
        compiler_params=pltpu.CompilerParams(
            collective_id=0, has_side_effects=True, vmem_limit_bytes=55_200_000
        ),
    )(
        live_count.reshape(1), owner_rank.reshape(NB), owner_tile.reshape(NB),
        face_blocks.reshape(NB, BLK * BLK), right_side, diagonal,
    )


def solution(mesh):
    sizes = (mesh.shape["gx"], mesh.shape["gy"], mesh.shape["gz"])
    return jax.shard_map(
        functools.partial(per_device, sizes),
        mesh=mesh,
        in_specs=(
            P("gx", "gy", "gz", None, None),
            P("gx", "gy", "gz", None, None),
            P("gx", "gy", "gz", None),
            P("gx", "gy", "gz"),
            P("gx", "gy", "gz"),
            P("gx", "gy", "gz"),
        ),
        out_specs=(P("gx", "gy", "gz"), P("gx", "gy", "gz")),
        check_vma=False,
    )
```

time: 211 us -> 61 us (0.29)
  the two profiles are of different devices: /device:TPU:8 before, /device:TPU:1 now
where the time goes in v1:
time: 61 us; the launch traced here: 60.8 us
  Pallas kernels  56.7 us (93%)
  local copies, waits for them, and re-layouts  2.89 us (5%)
  between operations  1.29 us (2%)
    pallas_call x1, Pallas kernels, per_device(): pl.pallas_call(functools.partial(body, n_gx, n_gy, n_gz), out_shape=(jax....  56.7 us
    unnamed x6, local copies, waits for them, and re-layouts  2.89 us

profile of v1, /device:TPU:1, one launch (start us, length us, event | category | flops | bytes accessed | tf_op | source)
XLA Modules:
  0.0 60.8 jit_solution(7335999977720643400)
XLA Ops:
  1.3 0.0 copy-start
  1.3 0.6 %copy-done = s32[1,1,1,24,1]{3,4,2,1,0:T(1,128)S(1)} copy-done((s32[1,1,1,24,1]{3,4,2,1,0:T(1,128)S(1)}, s32[1,1,1,24,1]{3,4,2,1,0:T(1,128)}, u32[]{:S(2)}) %copy-start) | copy-done | bytes 120
  1.9 0.0 copy-start.1
  1.9 0.7 %copy-done.1 = s32[1,1,1,24]{3,2,1,0:T(1,128)S(1)} copy-done((s32[1,1,1,24]{3,2,1,0:T(1,128)S(1)}, s32[1,1,1,24]{3,2,1,0:T(1,128)}, u32[]{:S(2)}) %copy-start.1) | copy-done | bytes 120
  2.6 56.7 %shard_map.77 = (f32[16,64,128]{2,1,0:T(8,128)S(1)}, f32[16,64,128]{2,1,0:T(8,128)S(1)}) custom-call(s32[1]{0:T(128)} %bitcast.4.count_hbm, s32[24]{0:T(128)S(1)} %bitcast.5, s32[24]{0:T(128)S(1)} %bitcast.6, f32[24,16384]{1,0:T(8,128)} %bitcast.7, f32[16,64,128]{2,1,0:T(8,128)} %rhs_ref.1, f32[16,64,128]{2,1,0:T(8,128)} %diag_ref.1), custom_call_target="tpu_custom_call" | custom-call | tf_op jit(solution)/shard_map/pallas_call | solution.py:449
  59.3 0.8 %copy.11 = f32[16,64,128]{2,1,0:T(8,128)} copy(f32[16,64,128]{2,1,0:T(8,128)S(1)} %get-tuple-element.4) | data formatting | bytes 1048576
  60.0 0.8 %copy.12 = f32[16,64,128]{2,1,0:T(8,128)} copy(f32[16,64,128]{2,1,0:T(8,128)S(1)} %get-tuple-element.5) | data formatting | bytes 1048576
Async XLA Ops:
  1.3 0.7 %copy-start = (s32[1,1,1,24,1]{3,4,2,1,0:T(1,128)S(1)}, s32[1,1,1,24,1]{3,4,2,1,0:T(1,128)}, u32[]{:S(2)}) copy-start(s32[1,1,1,24,1]{3,4,2,1,0:T(1,128)} %param.7) | copy-start | bytes 292
  1.9 0.7 %copy-start.1 = (s32[1,1,1,24]{3,2,1,0:T(1,128)S(1)}, s32[1,1,1,24]{3,2,1,0:T(1,128)}, u32[]{:S(2)}) copy-start(s32[1,1,1,24]{3,2,1,0:T(1,128)} %param.8) | copy-start | bytes 292

commit v2 on v1

--- a/solution.py
+++ b/solution.py
@@ -13,7 +13,12 @@
 CX = 16
 F32 = jnp.float32
 MESH = pl.DeviceIdType.MESH
+SHIFT = 6.5
 TOP = 8
+
+
+def ring_offsets(n, d):
+    return tuple(sorted({d % n, -d % n} - {0}))
 
 
 def body(
@@ -23,7 +28,7 @@
     count_ref, rank_ref, tile_ref, live_rank, face, rows, pair, sbuf, rbuf, stag, rtag,
     v0, v1, v2, diag, ysend, yrecv, zsend, zrecv,
     part_a, part_b, recv_a, recv_b,
-    in_sem, s_sem, r_sem, st_sem, rt_sem, hs_sem, hr_sem,
+    known, in_sem, s_sem, r_sem, st_sem, rt_sem, hs_sem, hr_sem,
     as_sem, ar_sem, bs_sem, br_sem,
 ):
     gx, gy, gz = lax.axis_index("gx"), lax.axis_index("gy"), lax.axis_index("gz")
@@ -32,6 +37,38 @@
     plane_n = n_gy * n_gz
     plane_me = gy * n_gz + gz
     barrier = pltpu.get_barrier_semaphore()
+
+    def step_chip(t):
+        j = t // 2
+        return (1 - 2 * (j % 2)) * (chips // 2 - (j + 1) // 2)
+
+    def target_of(t):
+        return lax.rem(chip + step_chip(t) + chips, chips) * 2 + lax.rem(core + 1 + t, 2)
+
+    def source_of(t):
+        return lax.rem(chip - step_chip(t) + chips, chips) * 2 + lax.rem(core + 1 + t, 2)
+
+    zrecv[...] = jnp.zeros_like(zrecv)
+    yrecv[...] = jnp.zeros_like(yrecv)
+
+    near_y, near_z = ring_offsets(n_gy, 1), ring_offsets(n_gz, 1)
+    far_z = ring_offsets(n_gz, 2) if n_gz > 4 else ()
+
+    def along_y(k):
+        return (gx, lax.rem(gy + k, n_gy), gz)
+
+    def along_z(k):
+        return (gx, gy, lax.rem(gz + k, n_gz))
+
+    def tell(sem, peer):
+        pl.semaphore_signal(sem, inc=1, device_id=peer, device_id_type=MESH)
+
+    for t in range(n_gx - 1):
+        tell(barrier, (target_of(t), gy, gz))
+    for k in near_y:
+        tell(barrier, along_y(k))
+    for k in near_z:
+        tell(barrier, along_z(k))
 
     small_copies = [
         pltpu.make_async_copy(src, dst, in_sem.at[6 + i])
@@ -58,23 +95,9 @@
     diag_copy = pltpu.make_async_copy(diag_ref, diag, in_sem.at[pieces + 1])
     diag_copy.start()
 
-    zrecv[...] = jnp.zeros_like(zrecv)
-    yrecv[...] = jnp.zeros_like(yrecv)
-
-    @pl.loop(1, n_gx)
-    def _(k):
-        pl.semaphore_signal(
-            barrier, inc=1, device_id=(lax.rem(gx + k, n_gx), gy, gz), device_id_type=MESH
-        )
-
     def plane_peer(k):
         q = lax.rem(plane_me + k, plane_n)
         return q // n_gz, lax.rem(q, n_gz)
-
-    @pl.loop(1, plane_n)
-    def _(k):
-        py, pz = plane_peer(k)
-        pl.semaphore_signal(barrier, inc=1, device_id=(gx, py, pz), device_id_type=MESH)
 
     lane = lax.broadcasted_iota(jnp.int32, (8, BLK), 1)
     k_at = lax.broadcasted_iota(jnp.int32, (2 * BLK, BLK), 0)
@@ -89,8 +112,6 @@
     for s in range(NB):
         live_rank[s] = jnp.where(s < count, rank_ref[s], -1)
 
-    pl.semaphore_wait(barrier, n_gx - 1 + plane_n - 1)
-
     @pl.when(gx == 0)
     def _():
         for v in (v0, v1):
@@ -114,15 +135,11 @@
                 for g in range(NB // 8):
                     by_row[pl.ds(g * 8 * HALF + r, 8, stride=HALF), :] = both[g * 8 : g * 8 + 8]
 
-    def step_chip(t):
-        j = t // 2
-        return (1 - 2 * (j % 2)) * (chips // 2 - (j + 1) // 2)
-
-    def target_of(t):
-        return lax.rem(chip + step_chip(t) + chips, chips) * 2 + lax.rem(core + 1 + t, 2)
-
-    def source_of(t):
-        return lax.rem(chip - step_chip(t) + chips, chips) * 2 + lax.rem(core + 1 + t, 2)
+    pl.semaphore_wait(barrier, n_gx - 1 + len(near_y) + len(near_z))
+    for k in near_y:
+        tell(known.at[0], along_y(k))
+    for k in near_z:
+        tell(known.at[0], along_z(k))
 
     def packed(tgt):
         i0, i1 = jnp.int32(NB), jnp.int32(NB)
@@ -163,14 +180,24 @@
             device_id=(tgt, gy, gz), device_id_type=MESH,
         )
 
-    @pl.loop(0, n_gx - 1)
+    last = n_gx - 1
+
+    @pl.loop(0, n_gx)
     def _(t):
         tgt = target_of(t)
         o, tag = packed(tgt)
-        stag[t] = tag
-        sbuf[t] = o
-        tag_copy(t, tgt, gx).start()
-        tile_copy(t, tgt, gx).start()
+
+        @pl.when(t < last)
+        def _():
+            stag[t] = tag
+            sbuf[t] = o
+            tag_copy(t, tgt, gx).start()
+            tile_copy(t, tgt, gx).start()
+
+        @pl.when(t == last)
+        def _():
+            rtag[gx] = tag
+            rbuf[gx] = o
 
     def add_tiles(tile, tag):
         swapped = pltpu.roll(tile, HALF, 1)
@@ -190,17 +217,37 @@
                 v0[1 + x, pl.ds(TOP, HALF), :] = v0[1 + x, pl.ds(TOP, HALF), :] + more
 
     rhs_copy.wait()
-    own, own_tag = packed(gx)
-    add_tiles(own, own_tag)
-
-    @pl.loop(0, n_gx - 1)
-    def _(t):
+    pl.semaphore_wait(known.at[0], len(near_y) + len(near_z))
+    for k in far_z:
+        tell(known.at[1], along_z(k))
+
+    @pl.loop(0, n_gx)
+    def _(i):
+        t = lax.rem(i + last, n_gx)
         src = source_of(t)
-        tag_copy(t, src, src).wait_recv()
-        tile_copy(t, src, src).wait_recv()
+
+        @pl.when(t < last)
+        def _():
+            tag_copy(t, src, src).wait_recv()
+            tile_copy(t, src, src).wait_recv()
+
+        @pl.when(i == n_gx // 2)
+        def _():
+            if far_z:
+                pl.semaphore_wait(known.at[1], len(far_z))
+            for k in range(1, n_gy):
+                tell(known.at[2], along_y(k))
+
         add_tiles(rbuf[src], rtag[src])
 
+    if n_gy > 1:
+        pl.semaphore_wait(known.at[2], n_gy - 1)
     diag_copy.wait()
+
+    def total(refs):
+        while len(refs) > 1:
+            refs = [refs[i] + refs[i + 1] if i + 1 < len(refs) else refs[i] for i in range(0, len(refs), 2)]
+        return refs[0]
 
     ends = (lane == 0) | (lane == BLK - 1)
     even = lane % 2 == 0
@@ -273,21 +320,12 @@
             ysend[at, 1, pl.ds(p, 1), :] = v[1 + p, pl.ds(TOP + HALF - 1, 1), :]
         go(faces[2:4])
 
-        def gather(i, carry):
-            out = []
-            for u in range(2):
-                p = 2 * i + u
-                acc = None
-                for yb in range(HALF // 8):
-                    c = jnp.where(ends, v[1 + p, pl.ds(TOP + 8 * yb, 8), :], 0.0)
-                    if yb:
-                        c = pltpu.roll(c, 16 * yb, 1)
-                    acc = c if acc is None else acc + c
-                out.append(carry[u] + pltpu.roll(acc, p, 1))
-            return tuple(out)
-
-        zero = jnp.zeros((8, BLK), F32)
-        v_even, v_odd = lax.fori_loop(0, CX // 2, gather, (zero, zero))
+        parts = [[], []]
+        for p in range(CX):
+            for yb in range(HALF // 8):
+                c = jnp.where(ends, v[1 + p, pl.ds(TOP + 8 * yb, 8), :], 0.0)
+                parts[p % 2].append(pltpu.roll(c, 16 * yb + p, 1) if 16 * yb + p else c)
+        v_even, v_odd = total(parts[0]), total(parts[1])
         zsend[at, 0] = jnp.where(even, v_even, v_odd)
         zsend[at, 1] = jnp.where(even, v_odd, v_even)
         go(faces[4:])
@@ -306,24 +344,27 @@
     def apply(v, at, visit, sums):
         sides = take_faces(v, at)
 
+        step = 4
+
         def planes(i, sums):
-            for u in range(2):
-                p = 2 * i + u
-                side = pltpu.roll(sides[u], lax.rem(BLK - p, BLK), 1)
+            base = i * step
+            here = [pltpu.roll(side, lax.rem(BLK - base, BLK), 1) for side in sides]
+            for u in range(step):
+                p = base + u
                 for yb in range(HALF // 8):
-                    row = TOP + 8 * yb
-                    h = pltpu.roll(side, BLK - 16 * yb, 1) if yb else side
+                    row, k = TOP + 8 * yb, 16 * yb + u
+                    h = pltpu.roll(here[u % 2], BLK - k, 1) if k else here[0]
                     c = v[1 + p, pl.ds(row, 8), :]
                     near = v[p, pl.ds(row, 8), :] + v[2 + p, pl.ds(row, 8), :]
                     near = near + (v[1 + p, pl.ds(row - 1, 8), :] + v[1 + p, pl.ds(row + 1, 8), :])
                     z_low = pltpu.roll(jnp.where(lane == BLK - 1, h, c), 1, 1)
                     z_high = pltpu.roll(jnp.where(lane == 0, h, c), BLK - 1, 1)
                     near = near + (z_low + z_high)
-                    image = (6.0 + diag[p, pl.ds(8 * yb, 8), :]) * c - near
+                    image = (diag[p, pl.ds(8 * yb, 8), :] + (6.0 - SHIFT)) * c - near
                     sums = visit(p, yb, c, image, sums)
             return sums
 
-        return lax.fori_loop(0, CX // 2, planes, sums)
+        return lax.fori_loop(0, CX // step, planes, sums)
 
     zero = jnp.zeros((8, BLK), F32)
 
@@ -366,16 +407,22 @@
             device_id=(gx,) + peer, device_id_type=MESH,
         )
 
-    def total(refs):
-        while len(refs) > 1:
-            refs = [refs[i] + refs[i + 1] if i + 1 < len(refs) else refs[i] for i in range(0, len(refs), 2)]
-        return refs[0]
-
     @pl.loop(1, n_gx)
     def _(k):
         a_copy(k, lax.rem(gx + k, n_gx), gx).start()
 
     recv_a[gx] = mine[0:1]
+
+    @pl.loop(0, n_gx - 1)
+    def _(t):
+        tag_copy(t, target_of(t), gx).wait_send()
+        tile_copy(t, target_of(t), gx).wait_send()
+
+    for v, at in ((v0, 0), (v1, 1)):
+        for copy, sends, _ in halo(v, at):
+            @pl.when(sends)
+            def _():
+                copy().wait_send()
 
     @pl.loop(1, n_gx)
     def _(k):
@@ -390,6 +437,14 @@
         b_copy(k, plane_peer(k), plane_me).start()
 
     recv_b[plane_me] = stage
+
+    @pl.loop(1, n_gx)
+    def _(k):
+        a_copy(k, lax.rem(gx + k, n_gx), gx).wait_send()
+
+    @pl.loop(1, plane_n)
+    def _(k):
+        b_copy(k, plane_peer(k), plane_me).wait_send()
 
     @pl.loop(1, plane_n)
     def _(k):
@@ -402,12 +457,16 @@
     m0, m1, m2, m3 = (
         jnp.broadcast_to(whole[:, 32 * q + 31 : 32 * q + 32], (8, BLK)) for q in range(4)
     )
-    alpha_0 = m0 / m1
-    square = alpha_0 * alpha_0
-    grown = square * m2 / m0
-    alpha_1 = (grown - 1.0) * m0 / (square * m3 - grown * grown * m1)
-    c0 = alpha_0 + alpha_1 * grown
-    c1 = alpha_0 * alpha_1
+    e = m1 / m0
+    a0 = 1.0 / (SHIFT + e)
+    s = m2 - e * m1
+    grow = a0 * s / m0
+    a1 = 1.0 / (SHIFT + (m3 - 2.0 * e * m2 + e * e * m1) / s - grow)
+    b0 = a0 * grow
+    x0 = a0 + a1 * (b0 + a0 * e)
+    x1 = a1 * a0
+    r0 = a0 * e * (1.0 - a1 * SHIFT) - a1 * b0 * SHIFT
+    r1 = a0 * (a1 * (SHIFT - e) - 1.0) - a1 * b0
 
     @pl.loop(0, CX)
     def _(p):
@@ -415,27 +474,8 @@
             a = v0[1 + p, pl.ds(TOP + 8 * yb, 8), :]
             b = v1[1 + p, pl.ds(TOP + 8 * yb, 8), :]
             c = v2[p, pl.ds(8 * yb, 8), :]
-            x_out[p, pl.ds(8 * yb, 8), :] = c0 * a - c1 * b
-            r_out[p, pl.ds(8 * yb, 8), :] = a - c0 * b + c1 * c
-
-    @pl.loop(0, n_gx - 1)
-    def _(t):
-        tag_copy(t, target_of(t), gx).wait_send()
-        tile_copy(t, target_of(t), gx).wait_send()
-
-    for v, at in ((v0, 0), (v1, 1)):
-        for copy, sends, _ in halo(v, at):
-            @pl.when(sends)
-            def _():
-                copy().wait_send()
-
-    @pl.loop(1, n_gx)
-    def _(k):
-        a_copy(k, lax.rem(gx + k, n_gx), gx).wait_send()
-
-    @pl.loop(1, plane_n)
-    def _(k):
-        b_copy(k, plane_peer(k), plane_me).wait_send()
+            x_out[p, pl.ds(8 * yb, 8), :] = x0 * a - x1 * b
+            r_out[p, pl.ds(8 * yb, 8), :] = r0 * a + (r1 * b + x1 * c)
 
 
 def per_device(sizes, face_blocks, owner_rank, owner_tile, live_count, right_side, diagonal):
@@ -475,6 +515,7 @@
             scratch((1, BLK), F32),
             scratch((n_gx, 1, BLK), F32),
             scratch((plane_n, 1, BLK), F32),
+            pltpu.SemaphoreType.REGULAR((3,)),
             dma((9,)),
             dma((n_gx,)), dma((n_gx,)), dma((n_gx,)), dma((n_gx,)),
             dma((2, 6)), dma((2, 6)),

time: 61 us -> 54.8 us (0.90)
  Pallas kernels: 56.7 us -> 50.5 us
    pallas_call x1, Pallas kernels: 56.7 us -> 50.5 us  [per_device(): pl.pallas_call(functools.partial(body, n_gx, n_gy, n_gz), out_shape=(jax....]
where the time goes in v2:
time: 54.8 us; the launch traced here: 54.7 us
  Pallas kernels  50.5 us (92%)
  local copies, waits for them, and re-layouts  2.89 us (5%)
  between operations  1.29 us (2%)
    pallas_call x1, Pallas kernels, per_device(): pl.pallas_call(functools.partial(body, n_gx, n_gy, n_gz), out_shape=(jax....  50.5 us
    unnamed x6, local copies, waits for them, and re-layouts  2.89 us

profile of v2, /device:TPU:1, one launch (start us, length us, event | category | flops | bytes accessed | tf_op | source)
XLA Modules:
  0.0 54.7 jit_solution(1167647371944751050)
XLA Ops:
  1.3 0.0 copy-start
  1.3 0.6 %copy-done = s32[1,1,1,24,1]{3,4,2,1,0:T(1,128)S(1)} copy-done((s32[1,1,1,24,1]{3,4,2,1,0:T(1,128)S(1)}, s32[1,1,1,24,1]{3,4,2,1,0:T(1,128)}, u32[]{:S(2)}) %copy-start) | copy-done | bytes 120
  1.9 0.0 copy-start.1
  1.9 0.7 %copy-done.1 = s32[1,1,1,24]{3,2,1,0:T(1,128)S(1)} copy-done((s32[1,1,1,24]{3,2,1,0:T(1,128)S(1)}, s32[1,1,1,24]{3,2,1,0:T(1,128)}, u32[]{:S(2)}) %copy-start.1) | copy-done | bytes 120
  2.6 50.5 %shard_map.77 = (f32[16,64,128]{2,1,0:T(8,128)S(1)}, f32[16,64,128]{2,1,0:T(8,128)S(1)}) custom-call(s32[1]{0:T(128)} %bitcast.4.count_hbm, s32[24]{0:T(128)S(1)} %bitcast.5, s32[24]{0:T(128)S(1)} %bitcast.6, f32[24,16384]{1,0:T(8,128)} %bitcast.7, f32[16,64,128]{2,1,0:T(8,128)} %rhs_ref.1, f32[16,64,128]{2,1,0:T(8,128)} %diag_ref.1), custom_call_target="tpu_custom_call" | custom-call | tf_op jit(solution)/shard_map/pallas_call | solution.py:489
  53.1 0.8 %copy.11 = f32[16,64,128]{2,1,0:T(8,128)} copy(f32[16,64,128]{2,1,0:T(8,128)S(1)} %get-tuple-element.4) | data formatting | bytes 1048576
  53.9 0.8 %copy.12 = f32[16,64,128]{2,1,0:T(8,128)} copy(f32[16,64,128]{2,1,0:T(8,128)S(1)} %get-tuple-element.5) | data formatting | bytes 1048576
Async XLA Ops:
  1.3 0.7 %copy-start = (s32[1,1,1,24,1]{3,4,2,1,0:T(1,128)S(1)}, s32[1,1,1,24,1]{3,4,2,1,0:T(1,128)}, u32[]{:S(2)}) copy-start(s32[1,1,1,24,1]{3,4,2,1,0:T(1,128)} %param.7) | copy-start | bytes 292
  1.9 0.7 %copy-start.1 = (s32[1,1,1,24]{3,2,1,0:T(1,128)S(1)}, s32[1,1,1,24]{3,2,1,0:T(1,128)}, u32[]{:S(2)}) copy-start(s32[1,1,1,24]{3,2,1,0:T(1,128)} %param.8) | copy-start | bytes 292

commit v3 on v2

v3 whole, which is shorter than its diff:
```python
import functools

import jax
import jax.numpy as jnp
from jax import lax
from jax.experimental import pallas as pl
from jax.experimental.pallas import tpu as pltpu
from jax.sharding import PartitionSpec as P

NB = 24
BLK = 128
HALF = BLK // 2
CX = 16
F32 = jnp.float32
MESH = pl.DeviceIdType.MESH
SHIFT = 6.5
TOP = 16
TWO = 2


def ring_offsets(n, d):
    return tuple(sorted({d % n, -d % n} - {0}))


def body(
    n_gx, n_gy, n_gz,
    small_hbm, face_ref, rhs_ref, diag_ref,
    x_out, r_out,
    small, live_rank, face, rows, pair, sbuf, rbuf, stag, rtag,
    v0, v1, v2, diag, ysend, yrecv, zsend, zrecv, xy, xz, yz,
    dysend, dyrecv, dzsend, dzrecv,
    part_a, part_b, recv_a, recv_b,
    known, in_sem, s_sem, r_sem, st_sem, rt_sem, hs_sem, hr_sem, ds_sem, dr_sem,
    as_sem, ar_sem, bs_sem, br_sem,
):
    gx, gy, gz = lax.axis_index("gx"), lax.axis_index("gy"), lax.axis_index("gz")
    chips = n_gx // 2
    chip, core = gx // 2, gx % 2
    plane_n = n_gy * n_gz
    plane_me = gy * n_gz + gz
    barrier = pltpu.get_barrier_semaphore()

    def step_chip(t):
        j = t // 2
        return (1 - 2 * (j % 2)) * (chips // 2 - (j + 1) // 2)

    def target_of(t):
        return lax.rem(chip + step_chip(t) + chips, chips) * 2 + lax.rem(core + 1 + t, 2)

    def source_of(t):
        return lax.rem(chip - step_chip(t) + chips, chips) * 2 + lax.rem(core + 1 + t, 2)

    for edge in (zrecv, yrecv, xy, xz, yz, dyrecv):
        edge[...] = jnp.zeros_like(edge)

    near_y, near_z = ring_offsets(n_gy, 1), ring_offsets(n_gz, 1)
    far_z = ring_offsets(n_gz, 2) if n_gz > 4 else ()

    def along_y(k):
        return (gx, lax.rem(gy + k, n_gy), gz)

    def along_z(k):
        return (gx, gy, lax.rem(gz + k, n_gz))

    def tell(sem, peer):
        pl.semaphore_signal(sem, inc=1, device_id=peer, device_id_type=MESH)

    for t in range(n_gx - 1):
        tell(barrier, (target_of(t), gy, gz))
    for k in near_y:
        tell(barrier, along_y(k))
    for k in near_z:
        tell(barrier, along_z(k))

    small_copies = [pltpu.make_async_copy(small_hbm, small, in_sem.at[6])]
    for c in small_copies:
        c.start()
    pieces = 4
    width = face.shape[1] // pieces
    face_copies = [
        pltpu.make_async_copy(
            face_ref.at[:, pl.ds(i * width, width)], face.at[:, pl.ds(i * width, width)], in_sem.at[i]
        )
        for i in range(pieces)
    ]
    for c in face_copies:
        c.start()
    rhs_copy = pltpu.make_async_copy(
        rhs_ref, v0.at[pl.ds(TWO, CX), pl.ds(TOP, HALF), :], in_sem.at[pieces]
    )
    rhs_copy.start()
    diag_copy = pltpu.make_async_copy(
        diag_ref, diag.at[pl.ds(TWO, CX), pl.ds(TOP, HALF), :], in_sem.at[pieces + 1]
    )
    diag_copy.start()

    def out_in(t, n):
        return (1 - 2 * (t % 2)) * (n // 2 - (t + 1) // 2)

    def plane_peer(t):
        py = lax.rem(gy + out_in(t % n_gy, n_gy) + n_gy, n_gy)
        return py, lax.rem(gz + out_in(t // n_gy, n_gz) + n_gz, n_gz)

    lane = lax.broadcasted_iota(jnp.int32, (8, BLK), 1)
    k_at = lax.broadcasted_iota(jnp.int32, (2 * BLK, BLK), 0)
    c_at = lax.broadcasted_iota(jnp.int32, (2 * BLK, BLK), 1)
    hit = (k_at // BLK == c_at // HALF) & ((k_at % BLK) // 2 == c_at % HALF)
    pair[...] = jnp.where(hit, 0.25, 0.0).astype(jnp.bfloat16)
    rows[NB] = jnp.zeros((HALF, BLK), F32)
    by_row = rows.reshape((NB + 1) * HALF, BLK)
    inner = pl.ds(TOP, HALF)

    def clear_plane(v, at):
        v[at, inner, :] = jnp.zeros((HALF, BLK), F32)

    @pl.when(gx == 0)
    def _():
        clear_plane(v0, 1)

    @pl.when(gx == n_gx - 1)
    def _():
        clear_plane(v0, TWO + CX)

    per = HALF // pieces
    for i in range(pieces):
        face_copies[i].wait()

        @pl.loop(0, per // 4)
        def _(r4):
            for u in range(4):
                r = i * per + r4 * 4 + u
                at = pl.multiple_of(r * 2 * BLK, 2 * BLK)
                both = face[:, pl.ds(at, BLK)] + face[:, pl.ds(at + BLK, BLK)]
                for g in range(NB // 8):
                    by_row[pl.ds(g * 8 * HALF + r, 8, stride=HALF), :] = both[g * 8 : g * 8 + 8]

    for c in small_copies:
        c.wait()
    count = small[2 * NB]
    for s in range(NB):
        live_rank[s] = jnp.where(s < count, small[s], -1)

    pl.semaphore_wait(barrier, n_gx - 1 + len(near_y) + len(near_z))
    for k in near_y:
        tell(known.at[0], along_y(k))
    for k in near_z:
        tell(known.at[0], along_z(k))

    def packed(tgt):
        i0, i1 = jnp.int32(NB), jnp.int32(NB)
        l0, l1 = jnp.int32(0), jnp.int32(0)
        for s in range(NB):
            named = live_rank[s] == tgt
            label = small[NB + s] + 1
            free = i0 == NB
            first = named & free
            second = named & jnp.logical_not(free)
            i1 = jnp.where(second, s, i1)
            l1 = jnp.where(second, label, l1)
            i0 = jnp.where(first, s, i0)
            l0 = jnp.where(first, label, l0)
        a = rows[i0]
        b = rows[i1]
        w = jnp.concatenate([a, b], axis=1)
        hi = w.astype(jnp.bfloat16)
        rest = w - hi.astype(F32)
        mid = rest.astype(jnp.bfloat16)
        low = (rest - mid.astype(F32)).astype(jnp.bfloat16)
        s = pair[...]
        o = jnp.dot(hi, s, preferred_element_type=F32)
        o = o + jnp.dot(mid, s, preferred_element_type=F32)
        o = o + jnp.dot(low, s, preferred_element_type=F32)
        tag = jnp.where(lane[0:1] < HALF, l0, l1).astype(F32)
        return o, tag

    def tile_copy(t, tgt, slot):
        return pltpu.make_async_remote_copy(
            src_ref=sbuf.at[t], dst_ref=rbuf.at[slot], send_sem=s_sem.at[t], recv_sem=r_sem.at[slot],
            device_id=(tgt, gy, gz), device_id_type=MESH,
        )

    def tag_copy(t, tgt, slot):
        return pltpu.make_async_remote_copy(
            src_ref=stag.at[t], dst_ref=rtag.at[slot], send_sem=st_sem.at[t], recv_sem=rt_sem.at[slot],
            device_id=(tgt, gy, gz), device_id_type=MESH,
        )

    last = n_gx - 1

    @pl.loop(0, n_gx)
    def _(t):
        tgt = target_of(t)
        o, tag = packed(tgt)

        @pl.when(t < last)
        def _():
            stag[t] = tag
            sbuf[t] = o
            tag_copy(t, tgt, gx).start()
            tile_copy(t, tgt, gx).start()

        @pl.when(t == last)
        def _():
            rtag[gx] = tag
            rbuf[gx] = o

    def add_tiles(tile, tag):
        swapped = pltpu.roll(tile, HALF, 1)
        tag = jnp.broadcast_to(tag, (8, BLK))
        tag_swapped = pltpu.roll(tag, HALF, 1)[0:1]
        tag = tag[0:1]
        want = (lane[0:1] // HALF + 1).astype(F32)

        @pl.loop(0, CX // 4)
        def _(x4):
            for u in range(4):
                x = x4 * 4 + u
                here = want + (2 * x).astype(F32)
                m = jnp.broadcast_to(tag == here, (HALF, BLK))
                ms = jnp.broadcast_to(tag_swapped == here, (HALF, BLK))
                more = jnp.where(m, tile, 0.0) + jnp.where(ms, swapped, 0.0)
                v0[TWO + x, inner, :] = v0[TWO + x, inner, :] + more

    def total(refs):
        while len(refs) > 1:
            refs = [refs[i] + refs[i + 1] if i + 1 < len(refs) else refs[i] for i in range(0, len(refs), 2)]
        return refs[0]

    even = lane % 2 == 0
    fourth = lane % 4
    outer = (lane < 2) | (lane >= BLK - 2)

    def z_columns(v):
        parts = [[], [], [], []]
        for p in range(CX):
            for yb in range(HALF // 8):
                c = jnp.where(outer, v[TWO + p, pl.ds(TOP + 8 * yb, 8), :], 0.0)
                k = 16 * yb + p
                parts[p % 4].append(pltpu.roll(c, k, 1) if k else c)
        parts = [total(p) for p in parts]

        def pick(off):
            out = parts[0]
            for j in range(1, 4):
                out = jnp.where(fourth == (j + off) % 4, parts[j], out)
            return pltpu.roll(out, -off % BLK, 1) if off else out

        return pick(0), pick(1), pick(-2), pick(-1)

    def within(off):
        sends, takes = [], []
        for o, at, n in zip(off, (gx, gy, gz), (n_gx, n_gy, n_gz)):
            if o:
                sends.append(at > 0 if o < 0 else at < n - 1)
                takes.append(at < n - 1 if o < 0 else at > 0)
        return functools.reduce(jnp.logical_and, sends), functools.reduce(jnp.logical_and, takes)

    def message(off, src, dst, s_sem, r_sem):
        return pltpu.make_async_remote_copy(
            src_ref=src, dst_ref=dst, send_sem=s_sem, recv_sem=r_sem,
            device_id=(gx + off[0], gy + off[1], gz + off[2]), device_id_type=MESH,
        )

    def each(messages, s_sems, r_sems, what):
        for i, (off, src, dst) in messages:
            sends, takes = within(off)

            @pl.when(takes if what == "take" else sends)
            def _():
                m = message(off, src, dst, s_sems.at[i], r_sems.at[i])
                if what == "send":
                    m.start()
                elif what == "take":
                    m.wait_recv()
                else:
                    m.wait_send()

    ways = (-1, 1)
    diag_messages = list(enumerate(
        [((-1, 0, 0), diag.at[TWO, inner, :], diag.at[TWO + CX, inner, :]),
         ((1, 0, 0), diag.at[TWO + CX - 1, inner, :], diag.at[TWO - 1, inner, :])]
        + [((0, o, 0), dysend.at[i], dyrecv.at[i]) for i, o in enumerate(ways)]
        + [((0, 0, o), dzsend.at[i], dzrecv.at[i]) for i, o in enumerate(ways)]
    ))
    x_messages = [
        ((o, 0, 0), v0.at[src + deep, inner, :], v0.at[dst + deep, inner, :])
        for o, src, dst in ((-1, TWO, TWO + CX), (1, CX, 0))
        for deep in range(2)
    ]
    y_messages = [
        ((a, b, 0), ysend.at[j, 0, i * (CX - 1)], xy.at[i, j])
        for i, a in enumerate(ways) for j, b in enumerate(ways)
    ] + [((0, o, 0), ysend.at[i], yrecv.at[i]) for i, o in enumerate(ways)]
    z_messages = [
        ((a, 0, b), zsend.at[j, 0], xz.at[i, j])
        for i, a in enumerate(ways) for j, b in enumerate(ways)
    ] + [
        ((0, a, b), zsend.at[j, 0], yz.at[i, j])
        for i, a in enumerate(ways) for j, b in enumerate(ways)
    ] + [((0, 0, o), zsend.at[i], zrecv.at[i]) for i, o in enumerate(ways)]
    side_messages = list(enumerate(x_messages + y_messages + z_messages))
    n_x, n_y = len(x_messages), len(x_messages) + len(y_messages)

    diag_copy.wait()
    for p in range(CX):
        dysend[0, p] = diag[TWO + p, pl.ds(TOP, 1), :]
        dysend[1, p] = diag[TWO + p, pl.ds(TOP + HALF - 1, 1), :]
    first, _, _, final = z_columns(diag)
    dzsend[0] = first
    dzsend[1] = final
    each(diag_messages, ds_sem, dr_sem, "send")

    rhs_copy.wait()
    pl.semaphore_wait(known.at[0], len(near_y) + len(near_z))
    for k in far_z:
        tell(known.at[1], along_z(k))

    @pl.loop(0, n_gx)
    def _(i):
        t = lax.rem(i + last, n_gx)
        src = source_of(t)

        @pl.when(t < last)
        def _():
            tag_copy(t, src, src).wait_recv()
            tile_copy(t, src, src).wait_recv()

        @pl.when(i == n_gx // 2)
        def _():
            if far_z:
                pl.semaphore_wait(known.at[1], len(far_z))
            for k in range(1, n_gy):
                tell(known.at[2], along_y(k))

        add_tiles(rbuf[src], rtag[src])

    if n_gy > 1:
        pl.semaphore_wait(known.at[2], n_gy - 1)

    each(side_messages[:n_x], hs_sem, hr_sem, "send")
    for p in range(CX):
        for deep in range(2):
            ysend[0, deep, p] = v0[TWO + p, pl.ds(TOP + deep, 1), :]
            ysend[1, deep, p] = v0[TWO + p, pl.ds(TOP + HALF - 1 - deep, 1), :]
    each(side_messages[n_x:n_y], hs_sem, hr_sem, "send")
    z_first, z_second, z_third, z_final = z_columns(v0)
    zsend[0, 0], zsend[0, 1] = z_first, z_second
    zsend[1, 0], zsend[1, 1] = z_final, z_third
    each(side_messages[n_y:], hs_sem, hr_sem, "send")

    each(diag_messages, ds_sem, dr_sem, "take")
    each(side_messages, hs_sem, hr_sem, "take")

    low, high = pl.ds(TOP - 1, 1), pl.ds(TOP + HALF, 1)
    for p in range(CX):
        diag[TWO + p, high, :] = dyrecv[0, p]
        diag[TWO + p, low, :] = dyrecv[1, p]
        v0[TWO + p, high, :] = yrecv[0, 0, p]
        v0[TWO + p, pl.ds(TOP + HALF + 1, 1), :] = yrecv[0, 1, p]
        v0[TWO + p, low, :] = yrecv[1, 0, p]
        v0[TWO + p, pl.ds(TOP - 2, 1), :] = yrecv[1, 1, p]
    for i, plane in enumerate((TWO + CX, TWO - 1)):
        v0[plane, high, :] = xy[i, 0]
        v0[plane, low, :] = xy[i, 1]

    def sides_of(right, left):
        left = pltpu.roll(left, BLK - 1, 1)
        return jnp.where(even, right, left), jnp.where(even, left, right)

    def image_of(v, plane, row, h):
        c = v[plane, pl.ds(row, 8), :]
        near = v[plane - 1, pl.ds(row, 8), :] + v[plane + 1, pl.ds(row, 8), :]
        near = near + (v[plane, pl.ds(row - 1, 8), :] + v[plane, pl.ds(row + 1, 8), :])
        z_low = pltpu.roll(jnp.where(lane == BLK - 1, h, c), 1, 1)
        z_high = pltpu.roll(jnp.where(lane == 0, h, c), BLK - 1, 1)
        near = near + (z_low + z_high)
        return c, (diag[plane, pl.ds(row, 8), :] + (6.0 - SHIFT)) * c - near

    def turned(side, k):
        return pltpu.roll(side, BLK - k, 1) if k else side

    def apply(v, sides, below, above, visit, sums):
        step = 4

        def planes(i, sums):
            base = i * step

            def moved(pair):
                return [pltpu.roll(side, lax.rem(BLK - base, BLK), 1) for side in pair]

            here = moved(sides)
            if below is not None:
                under, over = moved(below), moved(above)
            for u in range(step):
                p = base + u
                if below is not None:
                    _, image = image_of(v, TWO + p, TOP - 8, turned(under[u % 2], BLK - 16 + u))
                    v1[TWO + p, pl.ds(TOP - 8, 8), :] = image
                    _, image = image_of(v, TWO + p, TOP + HALF, turned(over[u % 2], u))
                    v1[TWO + p, pl.ds(TOP + HALF, 8), :] = image
                for yb in range(HALF // 8):
                    h = turned(here[u % 2], 16 * yb + u)
                    c, image = image_of(v, TWO + p, TOP + 8 * yb, h)
                    sums = visit(p, yb, c, image, sums)
            return sums

        return lax.fori_loop(0, CX // step, planes, sums)

    zero = jnp.zeros((8, BLK), F32)

    def visit_1(p, yb, c, image, sums):
        v1[TWO + p, pl.ds(TOP + 8 * yb, 8), :] = image
        return sums[0] + c * c, sums[1] + c * image, sums[2] + image * image

    def visit_2(p, yb, c, image, sums):
        v2[p, pl.ds(8 * yb, 8), :] = image
        return sums + c * image

    m0, m1, m2 = apply(
        v0, sides_of(zrecv[0, 0], zrecv[1, 0]), sides_of(yz[1, 0], yz[1, 1]),
        sides_of(yz[0, 0], yz[0, 1]), visit_1, (zero, zero, zero),
    )
    ring_planes = (
        (TWO + CX, 0, sides_of(xz[0, 0], xz[0, 1])[0]),
        (TWO - 1, CX - 1, sides_of(xz[1, 0], xz[1, 1])[1]),
    )
    for plane, p, side in ring_planes:
        for yb in range(HALF // 8):
            _, image = image_of(v0, plane, TOP + 8 * yb, turned(side, 16 * yb + p))
            v1[plane, pl.ds(TOP + 8 * yb, 8), :] = image
    row = lax.broadcasted_iota(jnp.int32, (8, BLK), 0)
    in_row = lane % CX

    def ring_columns(j, own, here):
        one, two = zrecv[j, 0], zrecv[j, 1]
        x_low = jnp.where(in_row == 0, pltpu.roll(xz[1, j], BLK - 15, 1), pltpu.roll(one, 1, 1))
        x_high = jnp.where(
            in_row == CX - 1, pltpu.roll(xz[0, j], 15, 1), pltpu.roll(one, BLK - 1, 1)
        )
        down, up = pltpu.roll(one, 1, 0), pltpu.roll(one, 7, 0)
        carried = jnp.where(lane >= BLK - CX, pltpu.roll(yz[1, j], 1, 0), down)
        y_low = jnp.where(row > 0, down, pltpu.roll(carried, CX, 1))
        carried = jnp.where(lane < CX, pltpu.roll(yz[0, j], 7, 0), up)
        y_high = jnp.where(row < 7, up, pltpu.roll(carried, BLK - CX, 1))
        near = (own + two) + (x_low + x_high) + (y_low + y_high)
        return jnp.where(here, (dzrecv[j] + (6.0 - SHIFT)) * one - near, 0.0)

    right = ring_columns(0, z_final, gz < n_gz - 1)
    left = ring_columns(1, z_first, gz > 0)

    @pl.when(gx == 0)
    def _():
        clear_plane(v1, TWO - 1)

    @pl.when(gx == n_gx - 1)
    def _():
        clear_plane(v1, TWO + CX)

    @pl.when(gy == 0)
    def _():
        for p in range(CX):
            v1[TWO + p, low, :] = jnp.zeros((1, BLK), F32)

    @pl.when(gy == n_gy - 1)
    def _():
        for p in range(CX):
            v1[TWO + p, high, :] = jnp.zeros((1, BLK), F32)

    m3 = apply(v1, sides_of(right, left), None, None, visit_2, zero)

    quarter = lane // 32
    folded = []
    for m in (m0, m1, m2, m3):
        m = m + pltpu.roll(m, 64, 1)
        folded.append(m + pltpu.roll(m, 32, 1))
    mine = jnp.where(
        quarter == 0, folded[0],
        jnp.where(quarter == 1, folded[1], jnp.where(quarter == 2, folded[2], folded[3])),
    )
    mine = mine + pltpu.roll(mine, 4, 0)
    mine = mine + pltpu.roll(mine, 2, 0)
    mine = mine + pltpu.roll(mine, 1, 0)
    part_a[...] = mine[0:1]

    def a_copy(k, peer, slot):
        return pltpu.make_async_remote_copy(
            src_ref=part_a, dst_ref=recv_a.at[slot], send_sem=as_sem.at[k], recv_sem=ar_sem.at[slot],
            device_id=(peer, gy, gz), device_id_type=MESH,
        )

    def b_copy(k, peer, slot):
        return pltpu.make_async_remote_copy(
            src_ref=part_b, dst_ref=recv_b.at[slot], send_sem=bs_sem.at[k], recv_sem=br_sem.at[slot],
            device_id=(gx,) + peer, device_id_type=MESH,
        )

    @pl.loop(0, n_gx - 1)
    def _(t):
        a_copy(t, target_of(t), gx).start()

    recv_a[gx] = mine[0:1]

    @pl.loop(0, n_gx - 1)
    def _(t):
        tag_copy(t, target_of(t), gx).wait_send()
        tile_copy(t, target_of(t), gx).wait_send()

    each(diag_messages, ds_sem, dr_sem, "sent")
    each(side_messages, hs_sem, hr_sem, "sent")

    @pl.loop(0, n_gx - 1)
    def _(t):
        src = source_of(t)
        a_copy(t, src, src).wait_recv()

    stage = total([recv_a[i] for i in range(n_gx)])
    part_b[...] = stage

    @pl.loop(0, plane_n - 1)
    def _(k):
        b_copy(k, plane_peer(k), plane_me).start()

    recv_b[plane_me] = stage

    @pl.loop(0, n_gx - 1)
    def _(t):
        a_copy(t, target_of(t), gx).wait_send()

    @pl.loop(0, plane_n - 1)
    def _(k):
        b_copy(k, plane_peer(k), plane_me).wait_send()

    @pl.loop(0, plane_n - 1)
    def _(k):
        py, pz = plane_peer(k)
        b_copy(k, (py, pz), py * n_gz + pz).wait_recv()

    whole = jnp.broadcast_to(total([recv_b[i] for i in range(plane_n)]), (8, BLK))
    for shift in (16, 8, 4, 2, 1):
        whole = whole + pltpu.roll(whole, shift, 1)
    m0, m1, m2, m3 = (
        jnp.broadcast_to(whole[:, 32 * q + 31 : 32 * q + 32], (8, BLK)) for q in range(4)
    )
    e = m1 / m0
    a0 = 1.0 / (SHIFT + e)
    s = m2 - e * m1
    grow = a0 * s / m0
    a1 = 1.0 / (SHIFT + (m3 - 2.0 * e * m2 + e * e * m1) / s - grow)
    b0 = a0 * grow
    x0 = a0 + a1 * (b0 + a0 * e)
    x1 = a1 * a0
    r0 = a0 * e * (1.0 - a1 * SHIFT) - a1 * b0 * SHIFT
    r1 = a0 * (a1 * (SHIFT - e) - 1.0) - a1 * b0

    @pl.loop(0, CX)
    def _(p):
        for yb in range(HALF // 8):
            a = v0[TWO + p, pl.ds(TOP + 8 * yb, 8), :]
            b = v1[TWO + p, pl.ds(TOP + 8 * yb, 8), :]
            c = v2[p, pl.ds(8 * yb, 8), :]
            x_out[p, pl.ds(8 * yb, 8), :] = x0 * a - x1 * b
            r_out[p, pl.ds(8 * yb, 8), :] = r0 * a + (r1 * b + x1 * c)


def per_device(sizes, face_blocks, owner_rank, owner_tile, live_count, right_side, diagonal):
    n_gx, n_gy, n_gz = sizes
    plane_n = n_gy * n_gz
    box = (CX, HALF, BLK)
    padded = (CX + 2 * TWO, HALF + 2 * TOP, BLK)
    vmem = pl.BlockSpec(memory_space=pltpu.VMEM)
    hbm = pl.BlockSpec(memory_space=pltpu.HBM)
    counts = jnp.broadcast_to(live_count.reshape(1), (BLK - 2 * NB,))
    small = jnp.concatenate([owner_rank.reshape(NB), owner_tile.reshape(NB), counts])
    dma, scratch = pltpu.SemaphoreType.DMA, pltpu.VMEM
    return pl.pallas_call(
        functools.partial(body, n_gx, n_gy, n_gz),
        out_shape=(jax.ShapeDtypeStruct(box, F32), jax.ShapeDtypeStruct(box, F32)),
        in_specs=[hbm] * 4,
        out_specs=(vmem, vmem),
        scratch_shapes=[
            pltpu.SMEM((BLK,), jnp.int32),
            pltpu.SMEM((NB,), jnp.int32),
            scratch((NB, BLK * BLK), F32),
            scratch((NB + 1, HALF, BLK), F32),
            scratch((2 * BLK, BLK), jnp.bfloat16),
            scratch((n_gx, HALF, BLK), F32),
            scratch((n_gx, HALF, BLK), F32),
            scratch((n_gx, 1, BLK), F32),
            scratch((n_gx, 1, BLK), F32),
            scratch(padded, F32),
            scratch(padded, F32),
            scratch(box, F32),
            scratch(padded, F32),
            scratch((2, 2, CX, 1, BLK), F32),
            scratch((2, 2, CX, 1, BLK), F32),
            scratch((2, 2, 8, BLK), F32),
            scratch((2, 2, 8, BLK), F32),
            scratch((2, 2, 1, BLK), F32),
            scratch((2, 2, 8, BLK), F32),
            scratch((2, 2, 8, BLK), F32),
            scratch((2, CX, 1, BLK), F32),
            scratch((2, CX, 1, BLK), F32),
            scratch((2, 8, BLK), F32),
            scratch((2, 8, BLK), F32),
            scratch((1, BLK), F32),
            scratch((1, BLK), F32),
            scratch((n_gx, 1, BLK), F32),
            scratch((plane_n, 1, BLK), F32),
            pltpu.SemaphoreType.REGULAR((3,)),
            dma((9,)),
            dma((n_gx,)), dma((n_gx,)), dma((n_gx,)), dma((n_gx,)),
            dma((20,)), dma((20,)), dma((6,)), dma((6,)),
            dma((n_gx,)), dma((n_gx,)), dma((plane_n,)), dma((plane_n,)),
        ],
        compiler_params=pltpu.CompilerParams(
            collective_id=0, has_side_effects=True, vmem_limit_bytes=55_200_000
        ),
    )(
        small,
        face_blocks.reshape(NB, BLK * BLK), right_side, diagonal,
    )


def solution(mesh):
    sizes = (mesh.shape["gx"], mesh.shape["gy"], mesh.shape["gz"])
    return jax.shard_map(
        functools.partial(per_device, sizes),
        mesh=mesh,
        in_specs=(
            P("gx", "gy", "gz", None, None),
            P("gx", "gy", "gz", None, None),
            P("gx", "gy", "gz", None),
            P("gx", "gy", "gz"),
            P("gx", "gy", "gz"),
            P("gx", "gy", "gz"),
        ),
        out_specs=(P("gx", "gy", "gz"), P("gx", "gy", "gz")),
        check_vma=False,
    )
```

time: 54.8 us -> 53 us (0.967)
  local copies, waits for them, and re-layouts: 2.89 us -> 1.59 us
  Pallas kernels: 50.5 us -> 49.2 us
  other arithmetic: 0 us -> 0.75 us
    unnamed x6 -> x2, local copies, waits for them, and re-layouts: 2.89 us -> 1.59 us
    pallas_call x1, Pallas kernels: 50.5 us -> 49.2 us  [per_device(): pl.pallas_call(functools.partial(body, n_gx, n_gy, n_gz), out_shape=(jax....]
    concatenate x0 -> x1, other arithmetic: none -> 0.75 us  [per_device(): jnp.concatenate([owner_rank.reshape(NB), owner_tile.reshape(NB), counts])]
where the time goes in v3:
time: 53 us; the launch traced here: 52.9 us
  Pallas kernels  49.2 us (93%)
  local copies, waits for them, and re-layouts  1.59 us (3%)
  between operations  1.29 us (2%)
  other arithmetic  0.75 us (1%)
    pallas_call x1, Pallas kernels, per_device(): pl.pallas_call(functools.partial(body, n_gx, n_gy, n_gz), out_shape=(jax....  49.2 us
    unnamed x2, local copies, waits for them, and re-layouts  1.59 us

profile of v3, /device:TPU:1, one launch (start us, length us, event | category | flops | bytes accessed | tf_op | source)
XLA Modules:
  0.0 52.9 jit_solution(17504270673765566742)
XLA Ops:
  1.3 0.8 %pad_add_fusion.small_hbm = s32[128]{0:T(128)S(1)} fusion(s32[80]{0:T(128)S(1)} %broadcast_in_dim.8, s32[24]{0:T(128)} %bitcast.6, s32[24]{0:T(128)} %bitcast.7), kind=kLoop, calls=%fused_computation | loop fusion | flops 256 | bytes 1024 | tf_op jit(solution)/shard_map/concatenate | solution.py:573
  2.0 49.2 %shard_map.77 = (f32[16,64,128]{2,1,0:T(8,128)S(1)}, f32[16,64,128]{2,1,0:T(8,128)S(1)}) custom-call(s32[128]{0:T(128)S(1)} %pad_add_fusion.small_hbm, f32[24,16384]{1,0:T(8,128)} %bitcast.5, f32[16,64,128]{2,1,0:T(8,128)} %rhs_ref.1, f32[16,64,128]{2,1,0:T(8,128)} %diag_ref.1), custom_call_target="tpu_custom_call" | custom-call | tf_op jit(solution)/shard_map/pallas_call | solution.py:575
  51.3 0.8 %copy.11 = f32[16,64,128]{2,1,0:T(8,128)} copy(f32[16,64,128]{2,1,0:T(8,128)S(1)} %get-tuple-element.4) | data formatting | bytes 1048576
  52.1 0.8 %copy.12 = f32[16,64,128]{2,1,0:T(8,128)} copy(f32[16,64,128]{2,1,0:T(8,128)S(1)} %get-tuple-element.5) | data formatting | bytes 1048576
  (1 shorter events, 0.0 us)

commit v4 on v3

--- a/solution.py
+++ b/solution.py
@@ -25,9 +25,9 @@
 def body(
     n_gx, n_gy, n_gz,
     small_hbm, face_ref, rhs_ref, diag_ref,
-    x_out, r_out,
+    v0_out, v1_out, v2, x0_out, x1_out, r0_out, r1_out, r2_out,
     small, live_rank, face, rows, pair, sbuf, rbuf, stag, rtag,
-    v0, v1, v2, diag, ysend, yrecv, zsend, zrecv, xy, xz, yz,
+    v0, v1, diag, ysend, yrecv, zsend, zrecv, xy, xz, yz,
     dysend, dyrecv, dzsend, dzrecv,
     part_a, part_b, recv_a, recv_b,
     known, in_sem, s_sem, r_sem, st_sem, rt_sem, hs_sem, hr_sem, ds_sem, dr_sem,
@@ -379,25 +379,18 @@
     def turned(side, k):
         return pltpu.roll(side, BLK - k, 1) if k else side
 
-    def apply(v, sides, below, above, visit, sums):
-        step = 4
+    step = 8
+
+    def moved(pair, base):
+        return [pltpu.roll(side, lax.rem(BLK - base, BLK), 1) for side in pair]
+
+    def apply(v, sides, visit, sums):
 
         def planes(i, sums):
             base = i * step
-
-            def moved(pair):
-                return [pltpu.roll(side, lax.rem(BLK - base, BLK), 1) for side in pair]
-
-            here = moved(sides)
-            if below is not None:
-                under, over = moved(below), moved(above)
+            here = moved(sides, base)
             for u in range(step):
                 p = base + u
-                if below is not None:
-                    _, image = image_of(v, TWO + p, TOP - 8, turned(under[u % 2], BLK - 16 + u))
-                    v1[TWO + p, pl.ds(TOP - 8, 8), :] = image
-                    _, image = image_of(v, TWO + p, TOP + HALF, turned(over[u % 2], u))
-                    v1[TWO + p, pl.ds(TOP + HALF, 8), :] = image
                 for yb in range(HALF // 8):
                     h = turned(here[u % 2], 16 * yb + u)
                     c, image = image_of(v, TWO + p, TOP + 8 * yb, h)
@@ -410,6 +403,8 @@
 
     def visit_1(p, yb, c, image, sums):
         v1[TWO + p, pl.ds(TOP + 8 * yb, 8), :] = image
+        v0_out[p, pl.ds(8 * yb, 8), :] = c
+        v1_out[p, pl.ds(8 * yb, 8), :] = image
         return sums[0] + c * c, sums[1] + c * image, sums[2] + image * image
 
     def visit_2(p, yb, c, image, sums):
@@ -417,9 +412,21 @@
         return sums + c * image
 
     m0, m1, m2 = apply(
-        v0, sides_of(zrecv[0, 0], zrecv[1, 0]), sides_of(yz[1, 0], yz[1, 1]),
-        sides_of(yz[0, 0], yz[0, 1]), visit_1, (zero, zero, zero),
-    )
+        v0, sides_of(zrecv[0, 0], zrecv[1, 0]), visit_1, (zero, zero, zero)
+    )
+    below, above = sides_of(yz[1, 0], yz[1, 1]), sides_of(yz[0, 0], yz[0, 1])
+
+    @pl.loop(0, CX // step)
+    def _(i):
+        base = i * step
+        under, over = moved(below, base), moved(above, base)
+        for u in range(step):
+            p = base + u
+            _, image = image_of(v0, TWO + p, TOP - 8, turned(under[u % 2], BLK - 16 + u))
+            v1[TWO + p, pl.ds(TOP - 8, 8), :] = image
+            _, image = image_of(v0, TWO + p, TOP + HALF, turned(over[u % 2], u))
+            v1[TWO + p, pl.ds(TOP + HALF, 8), :] = image
+
     ring_planes = (
         (TWO + CX, 0, sides_of(xz[0, 0], xz[0, 1])[0]),
         (TWO - 1, CX - 1, sides_of(xz[1, 0], xz[1, 1])[1]),
@@ -466,7 +473,7 @@
         for p in range(CX):
             v1[TWO + p, high, :] = jnp.zeros((1, BLK), F32)
 
-    m3 = apply(v1, sides_of(right, left), None, None, visit_2, zero)
+    m3 = apply(v1, sides_of(right, left), visit_2, zero)
 
     quarter = lane // 32
     folded = []
@@ -552,14 +559,8 @@
     r0 = a0 * e * (1.0 - a1 * SHIFT) - a1 * b0 * SHIFT
     r1 = a0 * (a1 * (SHIFT - e) - 1.0) - a1 * b0
 
-    @pl.loop(0, CX)
-    def _(p):
-        for yb in range(HALF // 8):
-            a = v0[TWO + p, pl.ds(TOP + 8 * yb, 8), :]
-            b = v1[TWO + p, pl.ds(TOP + 8 * yb, 8), :]
-            c = v2[p, pl.ds(8 * yb, 8), :]
-            x_out[p, pl.ds(8 * yb, 8), :] = x0 * a - x1 * b
-            r_out[p, pl.ds(8 * yb, 8), :] = r0 * a + (r1 * b + x1 * c)
+    for out, w in ((x0_out, x0), (x1_out, -x1), (r0_out, r0), (r1_out, r1), (r2_out, x1)):
+        out[...] = w[0:1]
 
 
 def per_device(sizes, face_blocks, owner_rank, owner_tile, live_count, right_side, diagonal):
@@ -572,11 +573,11 @@
     counts = jnp.broadcast_to(live_count.reshape(1), (BLK - 2 * NB,))
     small = jnp.concatenate([owner_rank.reshape(NB), owner_tile.reshape(NB), counts])
     dma, scratch = pltpu.SemaphoreType.DMA, pltpu.VMEM
-    return pl.pallas_call(
+    v0, v1, v2, *weights = pl.pallas_call(
         functools.partial(body, n_gx, n_gy, n_gz),
-        out_shape=(jax.ShapeDtypeStruct(box, F32), jax.ShapeDtypeStruct(box, F32)),
+        out_shape=tuple(jax.ShapeDtypeStruct(shape, F32) for shape in (box,) * 3 + ((1, BLK),) * 5),
         in_specs=[hbm] * 4,
-        out_specs=(vmem, vmem),
+        out_specs=(vmem,) * 8,
         scratch_shapes=[
             pltpu.SMEM((BLK,), jnp.int32),
             pltpu.SMEM((NB,), jnp.int32),
@@ -589,7 +590,6 @@
             scratch((n_gx, 1, BLK), F32),
             scratch(padded, F32),
             scratch(padded, F32),
-            scratch(box, F32),
             scratch(padded, F32),
             scratch((2, 2, CX, 1, BLK), F32),
             scratch((2, 2, CX, 1, BLK), F32),
@@ -613,12 +613,14 @@
             dma((n_gx,)), dma((n_gx,)), dma((plane_n,)), dma((plane_n,)),
         ],
         compiler_params=pltpu.CompilerParams(
-            collective_id=0, has_side_effects=True, vmem_limit_bytes=55_200_000
+            collective_id=0, has_side_effects=True, vmem_limit_bytes=54_750_000
         ),
     )(
         small,
         face_blocks.reshape(NB, BLK * BLK), right_side, diagonal,
     )
+    x0, x1, r0, r1, r2 = (w.reshape(1, 1, BLK) for w in weights)
+    return x0 * v0 + x1 * v1, r0 * v0 + (r1 * v1 + r2 * v2)
 
 
 def solution(mesh):

time: 53 us -> 52 us (0.981)
  local copies, waits for them, and re-layouts: 1.59 us -> 0.01 us
  other arithmetic: 0.75 us -> 1.95 us
  Pallas kernels: 49.2 us -> 48.6 us
    unnamed x2 -> x0, local copies, waits for them, and re-layouts: 1.59 us -> none
    add x0 -> x1, other arithmetic: none -> 1.2 us  [per_device(): return (x0 * v0 + x1 * v1, r0 * v0 + (r1 * v1 + r2 * v2))]
    pallas_call x1, Pallas kernels: 49.2 us -> 48.6 us  [per_device(): pl.pallas_call(functools.partial(body, n_gx, n_gy, n_gz), out_shape=tuple...]
where the time goes in v4:
time: 52 us; the launch traced here: 51.9 us
  Pallas kernels  48.6 us (93%)
  other arithmetic  1.95 us (4%)
  between operations  1.29 us (2%)
    pallas_call x1, Pallas kernels, per_device(): pl.pallas_call(functools.partial(body, n_gx, n_gy, n_gz), out_shape=tuple...  48.6 us
    add x1, other arithmetic, per_device(): return (x0 * v0 + x1 * v1, r0 * v0 + (r1 * v1 + r2 * v2))  1.2 us

profile of v4, /device:TPU:1, one launch (start us, length us, event | category | flops | bytes accessed | tf_op | source)
XLA Modules:
  0.0 51.9 jit_solution(15325051546899158834)
XLA Ops:
  1.3 0.8 %pad_add_fusion.small_hbm = s32[128]{0:T(128)S(1)} fusion(s32[80]{0:T(128)S(1)} %broadcast_in_dim.8, s32[24]{0:T(128)} %bitcast.16, s32[24]{0:T(128)} %bitcast.17), kind=kLoop, calls=%fused_computation.2 | loop fusion | flops 256 | bytes 1024 | tf_op jit(solution)/shard_map/concatenate | solution.py:574
  2.0 48.6 %shard_map.77 = (f32[16,64,128]{2,1,0:T(8,128)S(1)}, f32[16,64,128]{2,1,0:T(8,128)S(1)}, f32[16,64,128]{2,1,0:T(8,128)S(1)}, f32[1,128]{1,0:T(1,128)S(1)}, f32[1...) custom-call(s32[128]{0:T(128)S(1)} %pad_add_fusion.small_hbm, ...), custom_call_target="tpu_custom_call" | custom-call | tf_op jit(solution)/shard_map/pallas_call | solution.py:576
  50.7 1.2 %add_add_fusion = (f32[16,64,128]{2,1,0:T(8,128)}, f32[16,64,128]{2,1,0:T(8,128)}) fusion(f32[16,64,128]{2,1,0:T(8,128)S(1)} %get-tuple-element.17, f32[16,64,128]{2,1,0:T(8,128)S(1)} %get-tuple-element.13, f32[16,64,128]{2,1,0:T(8,128)S(1)} %get-tuple-element.11, f32[128]{0:T(128)S(1)} %bitcast.14, f32[128]{0:T(128)S(1)} %bitcast.13, f32[128]{0:T(128)S(1)} %bitcast.12, ...), kind=kLoop, calls=%fused_computation | loop fusion | flops 1048576 | bytes 2624000 | tf_op jit(solution)/shard_map/add | solution.py:623
  (1 shorter events, 0.0 us)

commit v5 on v4

--- a/solution.py
+++ b/solution.py
@@ -109,6 +109,7 @@
     rows[NB] = jnp.zeros((HALF, BLK), F32)
     by_row = rows.reshape((NB + 1) * HALF, BLK)
     inner = pl.ds(TOP, HALF)
+    low, high = pl.ds(TOP - 1, 1), pl.ds(TOP + HALF, 1)
 
     def clear_plane(v, at):
         v[at, inner, :] = jnp.zeros((HALF, BLK), F32)
@@ -338,30 +339,25 @@
         pl.semaphore_wait(known.at[2], n_gy - 1)
 
     each(side_messages[:n_x], hs_sem, hr_sem, "send")
+    z_first, z_second, z_third, z_final = z_columns(v0)
+    zsend[0, 0], zsend[0, 1] = z_first, z_second
+    zsend[1, 0], zsend[1, 1] = z_final, z_third
+    each(side_messages[n_y:], hs_sem, hr_sem, "send")
     for p in range(CX):
         for deep in range(2):
             ysend[0, deep, p] = v0[TWO + p, pl.ds(TOP + deep, 1), :]
             ysend[1, deep, p] = v0[TWO + p, pl.ds(TOP + HALF - 1 - deep, 1), :]
     each(side_messages[n_x:n_y], hs_sem, hr_sem, "send")
-    z_first, z_second, z_third, z_final = z_columns(v0)
-    zsend[0, 0], zsend[0, 1] = z_first, z_second
-    zsend[1, 0], zsend[1, 1] = z_final, z_third
-    each(side_messages[n_y:], hs_sem, hr_sem, "send")
-
-    each(diag_messages, ds_sem, dr_sem, "take")
-    each(side_messages, hs_sem, hr_sem, "take")
-
-    low, high = pl.ds(TOP - 1, 1), pl.ds(TOP + HALF, 1)
+
+    faces = [m for m in side_messages if sum(map(abs, m[1][0])) == 1]
+    edges = [m for m in side_messages if sum(map(abs, m[1][0])) == 2]
+    each(faces, hs_sem, hr_sem, "take")
+
     for p in range(CX):
-        diag[TWO + p, high, :] = dyrecv[0, p]
-        diag[TWO + p, low, :] = dyrecv[1, p]
         v0[TWO + p, high, :] = yrecv[0, 0, p]
         v0[TWO + p, pl.ds(TOP + HALF + 1, 1), :] = yrecv[0, 1, p]
         v0[TWO + p, low, :] = yrecv[1, 0, p]
         v0[TWO + p, pl.ds(TOP - 2, 1), :] = yrecv[1, 1, p]
-    for i, plane in enumerate((TWO + CX, TWO - 1)):
-        v0[plane, high, :] = xy[i, 0]
-        v0[plane, low, :] = xy[i, 1]
 
     def sides_of(right, left):
         left = pltpu.roll(left, BLK - 1, 1)
@@ -414,6 +410,15 @@
     m0, m1, m2 = apply(
         v0, sides_of(zrecv[0, 0], zrecv[1, 0]), visit_1, (zero, zero, zero)
     )
+    each(diag_messages, ds_sem, dr_sem, "take")
+    for p in range(CX):
+        diag[TWO + p, high, :] = dyrecv[0, p]
+        diag[TWO + p, low, :] = dyrecv[1, p]
+    each(edges, hs_sem, hr_sem, "take")
+    for i, plane in enumerate((TWO + CX, TWO - 1)):
+        v0[plane, high, :] = xy[i, 0]
+        v0[plane, low, :] = xy[i, 1]
+
     below, above = sides_of(yz[1, 0], yz[1, 1]), sides_of(yz[0, 0], yz[0, 1])
 
     @pl.loop(0, CX // step)
@@ -516,9 +521,9 @@
     each(side_messages, hs_sem, hr_sem, "sent")
 
     @pl.loop(0, n_gx - 1)
-    def _(t):
-        src = source_of(t)
-        a_copy(t, src, src).wait_recv()
+    def _(i):
+        src = source_of(last - 1 - i)
+        a_copy(0, src, src).wait_recv()
 
     stage = total([recv_a[i] for i in range(n_gx)])
     part_b[...] = stage
@@ -538,9 +543,9 @@
         b_copy(k, plane_peer(k), plane_me).wait_send()
 
     @pl.loop(0, plane_n - 1)
-    def _(k):
-        py, pz = plane_peer(k)
-        b_copy(k, (py, pz), py * n_gz + pz).wait_recv()
+    def _(i):
+        py, pz = plane_peer(plane_n - 2 - i)
+        b_copy(0, (py, pz), py * n_gz + pz).wait_recv()
 
     whole = jnp.broadcast_to(total([recv_b[i] for i in range(plane_n)]), (8, BLK))
     for shift in (16, 8, 4, 2, 1):

time: 52 us -> 51.5 us (level)
    pallas_call x1, Pallas kernels: 48.6 us -> 48.1 us  [per_device(): pl.pallas_call(functools.partial(body, n_gx, n_gy, n_gz), out_shape=tuple...]
where the time goes in v5:
time: 51.5 us; the launch traced here: 51.3 us
  Pallas kernels  48.1 us (93%)
  other arithmetic  1.95 us (4%)
  between operations  1.29 us (3%)
    pallas_call x1, Pallas kernels, per_device(): pl.pallas_call(functools.partial(body, n_gx, n_gy, n_gz), out_shape=tuple...  48.1 us
    add x1, other arithmetic, per_device(): return (x0 * v0 + x1 * v1, r0 * v0 + (r1 * v1 + r2 * v2))  1.2 us

profile of v5, /device:TPU:1, one launch (start us, length us, event | category | flops | bytes accessed | tf_op | source)
XLA Modules:
  0.0 51.3 jit_solution(7182536626609340258)
XLA Ops:
  1.3 0.8 %pad_add_fusion.small_hbm = s32[128]{0:T(128)S(1)} fusion(s32[80]{0:T(128)S(1)} %broadcast_in_dim.8, s32[24]{0:T(128)} %bitcast.16, s32[24]{0:T(128)} %bitcast.17), kind=kLoop, calls=%fused_computation.2 | loop fusion | flops 256 | bytes 1024 | tf_op jit(solution)/shard_map/concatenate | solution.py:579
  2.0 48.1 %shard_map.77 = (f32[16,64,128]{2,1,0:T(8,128)S(1)}, f32[16,64,128]{2,1,0:T(8,128)S(1)}, f32[16,64,128]{2,1,0:T(8,128)S(1)}, f32[1,128]{1,0:T(1,128)S(1)}, f32[1...) custom-call(s32[128]{0:T(128)S(1)} %pad_add_fusion.small_hbm, ...), custom_call_target="tpu_custom_call" | custom-call | tf_op jit(solution)/shard_map/pallas_call | solution.py:581
  50.1 1.2 %add_add_fusion = (f32[16,64,128]{2,1,0:T(8,128)}, f32[16,64,128]{2,1,0:T(8,128)}) fusion(f32[16,64,128]{2,1,0:T(8,128)S(1)} %get-tuple-element.17, f32[16,64,128]{2,1,0:T(8,128)S(1)} %get-tuple-element.13, f32[16,64,128]{2,1,0:T(8,128)S(1)} %get-tuple-element.11, f32[128]{0:T(128)S(1)} %bitcast.14, f32[128]{0:T(128)S(1)} %bitcast.13, f32[128]{0:T(128)S(1)} %bitcast.12, ...), kind=kLoop, calls=%fused_computation | loop fusion | flops 1048576 | bytes 2624000 | tf_op jit(solution)/shard_map/add | solution.py:628
  (1 shorter events, 0.0 us)

commit v6 on v5

--- a/solution.py
+++ b/solution.py
@@ -26,11 +26,11 @@
     n_gx, n_gy, n_gz,
     small_hbm, face_ref, rhs_ref, diag_ref,
     v0_out, v1_out, v2, x0_out, x1_out, r0_out, r1_out, r2_out,
-    small, live_rank, face, rows, pair, sbuf, rbuf, stag, rtag,
+    small, live_rank, face, rows, pair, sbuf, rbuf,
     v0, v1, diag, ysend, yrecv, zsend, zrecv, xy, xz, yz,
     dysend, dyrecv, dzsend, dzrecv,
     part_a, part_b, recv_a, recv_b,
-    known, in_sem, s_sem, r_sem, st_sem, rt_sem, hs_sem, hr_sem, ds_sem, dr_sem,
+    known, in_sem, s_sem, r_sem, hs_sem, hr_sem, ds_sem, dr_sem,
     as_sem, ar_sem, bs_sem, br_sem,
 ):
     gx, gy, gz = lax.axis_index("gx"), lax.axis_index("gy"), lax.axis_index("gz")
@@ -174,15 +174,11 @@
         tag = jnp.where(lane[0:1] < HALF, l0, l1).astype(F32)
         return o, tag
 
+    with_tag = pl.ds(0, HALF + 1)
+
     def tile_copy(t, tgt, slot):
         return pltpu.make_async_remote_copy(
-            src_ref=sbuf.at[t], dst_ref=rbuf.at[slot], send_sem=s_sem.at[t], recv_sem=r_sem.at[slot],
-            device_id=(tgt, gy, gz), device_id_type=MESH,
-        )
-
-    def tag_copy(t, tgt, slot):
-        return pltpu.make_async_remote_copy(
-            src_ref=stag.at[t], dst_ref=rtag.at[slot], send_sem=st_sem.at[t], recv_sem=rt_sem.at[slot],
+            src_ref=sbuf.at[t, with_tag, :], dst_ref=rbuf.at[slot, with_tag, :], send_sem=s_sem.at[t], recv_sem=r_sem.at[slot],
             device_id=(tgt, gy, gz), device_id_type=MESH,
         )
 
@@ -195,15 +191,14 @@
 
         @pl.when(t < last)
         def _():
-            stag[t] = tag
-            sbuf[t] = o
-            tag_copy(t, tgt, gx).start()
+            sbuf[t, pl.ds(0, HALF), :] = o
+            sbuf[t, pl.ds(HALF, 1), :] = tag
             tile_copy(t, tgt, gx).start()
 
         @pl.when(t == last)
         def _():
-            rtag[gx] = tag
-            rbuf[gx] = o
+            rbuf[gx, pl.ds(0, HALF), :] = o
+            rbuf[gx, pl.ds(HALF, 1), :] = tag
 
     def add_tiles(tile, tag):
         swapped = pltpu.roll(tile, HALF, 1)
@@ -323,7 +318,6 @@
 
         @pl.when(t < last)
         def _():
-            tag_copy(t, src, src).wait_recv()
             tile_copy(t, src, src).wait_recv()
 
         @pl.when(i == n_gx // 2)
@@ -333,7 +327,7 @@
             for k in range(1, n_gy):
                 tell(known.at[2], along_y(k))
 
-        add_tiles(rbuf[src], rtag[src])
+        add_tiles(rbuf[src, pl.ds(0, HALF), :], rbuf[src, pl.ds(HALF, 1), :])
 
     if n_gy > 1:
         pl.semaphore_wait(known.at[2], n_gy - 1)
@@ -514,7 +508,6 @@
 
     @pl.loop(0, n_gx - 1)
     def _(t):
-        tag_copy(t, target_of(t), gx).wait_send()
         tile_copy(t, target_of(t), gx).wait_send()
 
     each(diag_messages, ds_sem, dr_sem, "sent")
@@ -589,10 +582,8 @@
             scratch((NB, BLK * BLK), F32),
             scratch((NB + 1, HALF, BLK), F32),
             scratch((2 * BLK, BLK), jnp.bfloat16),
-            scratch((n_gx, HALF, BLK), F32),
-            scratch((n_gx, HALF, BLK), F32),
-            scratch((n_gx, 1, BLK), F32),
-            scratch((n_gx, 1, BLK), F32),
+            scratch((n_gx, HALF + 8, BLK), F32),
+            scratch((n_gx, HALF + 8, BLK), F32),
             scratch(padded, F32),
             scratch(padded, F32),
             scratch(padded, F32),
@@ -613,7 +604,7 @@
             scratch((plane_n, 1, BLK), F32),
             pltpu.SemaphoreType.REGULAR((3,)),
             dma((9,)),
-            dma((n_gx,)), dma((n_gx,)), dma((n_gx,)), dma((n_gx,)),
+            dma((n_gx,)), dma((n_gx,)),
             dma((20,)), dma((20,)), dma((6,)), dma((6,)),
             dma((n_gx,)), dma((n_gx,)), dma((plane_n,)), dma((plane_n,)),
         ],

time: 51.5 us -> 51.2 us (level)
  no operation moved by 1% of the time
where the time goes in v6:
time: 51.2 us; the launch traced here: 51 us
  Pallas kernels  47.8 us (93%)
  other arithmetic  1.95 us (4%)
  between operations  1.29 us (3%)
    pallas_call x1, Pallas kernels, per_device(): pl.pallas_call(functools.partial(body, n_gx, n_gy, n_gz), out_shape=tuple...  47.8 us
    add x1, other arithmetic, per_device(): return (x0 * v0 + x1 * v1, r0 * v0 + (r1 * v1 + r2 * v2))  1.2 us

profile of v6, /device:TPU:1, one launch (start us, length us, event | category | flops | bytes accessed | tf_op | source)
XLA Modules:
  0.0 51.0 jit_solution(15193449044603918083)
XLA Ops:
  1.3 0.8 %pad_add_fusion.small_hbm = s32[128]{0:T(128)S(1)} fusion(s32[80]{0:T(128)S(1)} %broadcast_in_dim.8, s32[24]{0:T(128)} %bitcast.16, s32[24]{0:T(128)} %bitcast.17), kind=kLoop, calls=%fused_computation.2 | loop fusion | flops 256 | bytes 1024 | tf_op jit(solution)/shard_map/concatenate | solution.py:572
  2.0 47.8 %shard_map.77 = (f32[16,64,128]{2,1,0:T(8,128)S(1)}, f32[16,64,128]{2,1,0:T(8,128)S(1)}, f32[16,64,128]{2,1,0:T(8,128)S(1)}, f32[1,128]{1,0:T(1,128)S(1)}, f32[1...) custom-call(s32[128]{0:T(128)S(1)} %pad_add_fusion.small_hbm, ...), custom_call_target="tpu_custom_call" | custom-call | tf_op jit(solution)/shard_map/pallas_call | solution.py:574
  49.8 1.2 %add_add_fusion = (f32[16,64,128]{2,1,0:T(8,128)}, f32[16,64,128]{2,1,0:T(8,128)}) fusion(f32[16,64,128]{2,1,0:T(8,128)S(1)} %get-tuple-element.17, f32[16,64,128]{2,1,0:T(8,128)S(1)} %get-tuple-element.13, f32[16,64,128]{2,1,0:T(8,128)S(1)} %get-tuple-element.11, f32[128]{0:T(128)S(1)} %bitcast.14, f32[128]{0:T(128)S(1)} %bitcast.13, f32[128]{0:T(128)S(1)} %bitcast.12, ...), kind=kLoop, calls=%fused_computation | loop fusion | flops 1048576 | bytes 2624000 | tf_op jit(solution)/shard_map/add | solution.py:619
  (1 shorter events, 0.0 us)
